TPU v7x, 256 devices: a whole 4x4x8 slice. The times are simulated.
256 devices in a mesh: gx: 16 (over z, core), gy: 4 (over x), gz: 4 (over y).
Axes of the slice: x: 4, y: 4, z: 8, core: 2. Of those that a mesh axis runs over, the one named last changes fastest.
Arguments:
- block_values: bfloat16 [4, 64, 4, 6, 128, 128], P('gy', 'gx', 'gz'), as said below
- block_cols: int32 [4, 64, 4, 6], P('gy', 'gx', 'gz'), may hold values from 0 to 63, as said below
Outputs:
- purified: float32 [2048, 32768], P(('gx', 'gy'), 'gz')
Inputs may be any that keep to these rules, and one draw needn't show every extreme that they name: block_cols[a, s, b, :] holds 6 distinct tile columns of panel b at which tile row a * 64 + s of P is nonzero; every tile column of a panel is listed by exactly 6 tile rows of each slab; the pattern is symmetric: tile (i, j) is listed exactly when tile (j, i) is. `block_values`: P is symmetric: the tile listed at (i, j) is the transpose of the tile listed at (j, i), and diagonal tiles are symmetric.
All inputs are finite; a program needn't handle non-finite values.
Results may differ from a plain program's by a relative error of at most 0.0033.
Values may be sent and summed in bfloat16 or wider, within the bound.
A program may use at most 128 MiB of HBM per device.

v0:
```python
import jax
import jax.numpy as jnp
from jax import lax
from jax.sharding import PartitionSpec as P

WIN = 1


def picked_2(x, axis, root):
    return lax.dynamic_index_in_dim(lax.all_gather(x, axis), root, 0, keepdims=False)


def in_blocks(x, dim, length):
    lengths = x.shape
    tiles = x.reshape(*lengths[:dim], length, lengths[dim] // length, *lengths[dim + 1 :])
    return jnp.moveaxis(tiles, dim, 0)


def sent_and_summed(x, axis, dim):
    tiles = in_blocks(x, dim, lax.axis_size(axis))
    arrived = lax.all_to_all(tiles, axis, split_axis=0, concat_axis=0, tiled=True)
    return arrived.astype(jnp.float32).sum(axis=0)


def densify(left_tiles, left_columns, slab_tiles):
    onehot = (
        left_columns[:, :, None] == jnp.arange(slab_tiles, dtype=jnp.int32)[None, None, :]
    ).astype(jnp.bfloat16)
    densified = jnp.einsum("wkj,wkyx->wyjx", onehot, left_tiles, preferred_element_type=jnp.float32)
    tile_size = left_tiles.shape[2]
    return densified.astype(jnp.bfloat16).reshape(
        left_tiles.shape[0] * tile_size, slab_tiles, tile_size
    )


def product_one(left_panel, panel_tiles, panel_columns):
    summed = jnp.zeros(
        (left_panel.shape[0], panel_tiles.shape[0], panel_tiles.shape[2]), jnp.float32
    )
    for column_slot in range(panel_tiles.shape[1]):
        picked = jnp.take(left_panel, panel_columns[:, column_slot], axis=1)
        summed = summed + jnp.einsum(
            "rix,iyx->riy", picked, panel_tiles[:, column_slot], preferred_element_type=jnp.float32
        )
    return summed


def product_two(rounded, panel_tiles, panel_columns, panel_width):
    summed = jnp.zeros((rounded.shape[0], panel_width, panel_tiles.shape[3]), jnp.float32)
    for column_slot in range(panel_tiles.shape[1]):
        product = jnp.einsum(
            "rix,ixy->riy", rounded, panel_tiles[:, column_slot], preferred_element_type=jnp.float32
        )
        summed = summed.at[:, panel_columns[:, column_slot], :].add(product)
    return summed


def local(block_values, block_cols):
    tiles_here = block_values[0, :, 0]
    columns_here = block_cols[0, :, 0]
    tile_size = tiles_here.shape[2]
    slab_tiles = tiles_here.shape[0] * lax.axis_size("gx")
    left_tiles, left_columns = (
        picked_2(tiles_here[:WIN], "gy", 0),
        picked_2(columns_here[:WIN], "gy", 0),
    )
    left_panel = densify(left_tiles, left_columns, slab_tiles)
    height = left_panel.shape[0]
    on_diagonal = (lax.axis_index("gy") == lax.axis_index("gz")).astype(jnp.float32)
    panel_tiles, panel_columns = (
        lax.all_gather(tiles_here, "gx", axis=0, tiled=True),
        lax.all_gather(columns_here, "gx", axis=0, tiled=True),
    )
    partial_square = product_one(left_panel, panel_tiles, panel_columns)
    partial_square = partial_square.reshape(height, slab_tiles * tile_size)
    square = lax.psum(partial_square, "gz")
    square_low = square.astype(jnp.bfloat16).reshape(height, slab_tiles, tile_size)
    applied = product_two(square_low, panel_tiles, panel_columns, slab_tiles).reshape(
        height // lax.axis_size("gy") * lax.axis_size("gy"), slab_tiles * tile_size
    )
    return sent_and_summed(
        (3.0 * on_diagonal * square - 2.0 * applied).astype(jnp.bfloat16), "gy", 0
    )


def solution(mesh):
    in_specs = (P("gy", "gx", "gz", None, None, None), P("gy", "gx", "gz", None))
    out_specs = P(("gx", "gy"), "gz")
    return jax.shard_map(local, mesh=mesh, in_specs=in_specs, out_specs=out_specs, check_vma=False)
```

profile of v0, /device:TPU:1, one launch (start us, length us, event | category | flops | bytes accessed | tf_op | source)
XLA Modules:
  0.0 381.5 jit_solution(5912386459244780532)
XLA Ops:
  6.5 0.0 all-gather.6.cloned.1.call-start
  6.5 2.2 copy.30
  8.7 0.0 all-gather.6.cloned.1.call-update
  8.7 0.0 all-reduce.2.cloned.1.call-start
  8.8 8.5 %all-gather = s32[4,1,1,6]{3,2,1,0:T(1,128)S(1)} all-gather(s32[1,1,1,6]{3,2,1,0:T(1,128)S(1)} %slice-done.4), channel_id=2, replica_groups=mesh['gx'=16,'gy'=4,'gz'=4] {'gy'}, dimensions={0}, use_global_device_ids=true | all-gather | bytes 120 | tf_op jit(solution)/shard_map/all_gather | solution.py:10
  17.3 0.0 slice-done.3
  17.3 12.4 %all-gather.1 = bf16[4,1,1,6,128,128]{5,4,3,2,1,0:T(8,128)(2,1)S(1)} all-gather(bf16[1,1,1,6,128,128]{5,4,3,2,1,0:T(8,128)(2,1)S(1)} %slice-done.3), channel_id=3, replica_groups=mesh['gx'=16,'gy'=4,'gz'=4] {'gy'}, dimensions={0}, use_global_device_ids=true | all-gather | bytes 983040 | tf_op jit(solution)/shard_map/all_gather | solution.py:10
  29.7 0.8 convert_bitcast_fusion
  30.6 0.0 copy-start.5
  30.6 1.4 copy.29
  32.0 24.1 %all-gather.2 = s32[1,64,1,6]{3,2,0,1:T(1,128)S(1)} all-gather(s32[1,4,1,6]{3,2,0,1:T(1,128)S(1)} %bitcast.101), channel_id=4, replica_groups=mesh['gx'=16,'gy'=4,'gz'=4] {'gx'}, dimensions={1}, use_global_device_ids=true | all-gather | bytes 1632 | tf_op jit(solution)/shard_map/all_gather | solution.py:72
  56.1 0.4 fusion.41
  56.5 2.2 gather_fusion
  58.7 2.1 gather_fusion.4
  60.8 2.2 gather_fusion.3
  63.0 2.1 gather_fusion.2
  65.2 2.2 gather_fusion.1
  67.3 2.1 gather_fusion.5
  69.5 19.7 %all-gather.6.cloned.1.call-done = bf16[1,64,1,6,128,128]{5,4,1,3,2,0:T(8,128)(2,1)} async-done(((bf16[1,4,1,6,128,128]{5,4,1,3,2,0:T(8,128)(2,1)}), bf16[1,64,1,6,128,128]{5,4,1,3,2,0:T(8,128)(2,1)}) %all-gather.6.cloned.1.call-update) | async-done | bytes 12582928 | tf_op jit(solution)/shard_map/all_gather | solution.py:71
  89.2 6.2 %fusion.10 = f32[64,128,128]{1,2,0:T(8,128)} fusion(bf16[64,128,128]{2,1,0:T(8,128)(2,1)} %gather_fusion, pred[64]{0:T(512)(128)(4,1)S(1)} %get-tuple-element.29, bf16[64,6,128,128]{3,2,0,1:T(8,128)(2,1)} %bitcast.84), kind=kOutput, calls=%fused_computation.31 | convolution fusion | flops 269484032 | bytes 8388672 | tf_op jit(solution)/shard_map/rix,iyx->riy/dot_general | solution.py:42
  95.3 6.0 %fusion.2 = f32[64,128,128]{1,2,0:T(8,128)} fusion(bf16[64,128,128]{2,1,0:T(8,128)(2,1)} %gather_fusion.4, pred[64]{0:T(512)(128)(4,1)S(1)} %get-tuple-element.25, bf16[64,6,128,128]{3,2,0,1:T(8,128)(2,1)} %bitcast.85), kind=kOutput, calls=%fused_computation.23 | convolution fusion | flops 269484032 | bytes 8388672 | tf_op jit(solution)/shard_map/rix,iyx->riy/dot_general | solution.py:42
  101.3 3.6 fusion.4
  105.0 3.6 fusion.6
  108.6 3.6 fusion.8
  112.2 10.1 %add_add_fusion = f32[64,128,128]{1,2,0:T(8,128)} fusion(f32[64,128,128]{1,2,0:T(8,128)} %fusion.2, f32[64,128,128]{1,2,0:T(8,128)} %fusion.4, f32[64,128,128]{1,2,0:T(8,128)} %fusion.6, f32[64,128,128]{1,2,0:T(8,128)} %fusion.10, f32[64,128,128]{1,2,0:T(8,128)} %fusion.8, bf16[64,128,128]{2,1,0:T(8,128)(2,1)S(1)} %copy-done.4, ...), kind=kOutput, calls=%fused_computation.15 | convolution fusion | flops 274726912 | bytes 29360640 | tf_op jit(solution)/shard_map/rix,iyx->riy/dot_general | solution.py:42
  122.3 0.0 all-reduce.2.cloned.1.call-update
  122.3 96.0 %all-reduce.2.cloned.1.call-done = f32[128,8192]{0,1:T(8,128)} async-done(((f32[128,8192]{0,1:T(8,128)}), f32[128,8192]{0,1:T(8,128)}) %all-reduce.2.cloned.1.call-update) | async-done | bytes 4194320 | tf_op jit(solution)/shard_map/psum | solution.py:76
  218.4 2.5 convert_element_type.27
  220.9 0.0 slice-start.1
  220.9 4.6 %fusion.24 = f32[64,128,128]{2,1,0:T(8,128)} fusion(bf16[128,64,128]{0,2,1:T(8,128)(2,1)S(1)} %bitcast.78, bf16[64,6,128,128]{3,2,0,1:T(8,128)(2,1)} %bitcast.86), kind=kOutput, calls=%fused_computation.47 | convolution fusion | flops 268435456 | bytes 8388608 | tf_op jit(solution)/shard_map/rix,ixy->riy/dot_general | solution.py:51
  225.5 4.6 %fusion.25 = f32[64,128,128]{2,1,0:T(8,128)} fusion(bf16[128,64,128]{0,2,1:T(8,128)(2,1)S(1)} %bitcast.79, bf16[64,6,128,128]{3,2,0,1:T(8,128)(2,1)} %bitcast.87), kind=kOutput, calls=%fused_computation.48 | convolution fusion | flops 268435456 | bytes 8388608 | tf_op jit(solution)/shard_map/rix,ixy->riy/dot_general | solution.py:51
  230.1 2.8 fusion.26
  232.9 2.8 fusion.27
  235.7 2.8 fusion.28
  238.5 2.8 fusion.29
  241.3 2.5 broadcast_in_dim.11
  243.8 13.7 %scatter_fusion = f32[128,64,128]{2,0,1:T(8,128)} fusion(f32[128,64,128]{2,0,1:T(8,128)} %broadcast_in_dim.11, s32[64]{0:T(128)S(1)} %get-tuple-element.7, f32[64,128,128]{2,1,0:T(8,128)} %fusion.24), kind=kCustom, calls=%fused_computation.6 | custom fusion | flops 1048576 | bytes 12583168 | tf_op jit(solution)/shard_map/scatter-add | solution.py:54
  257.5 13.6 %scatter_fusion.1 = f32[128,64,128]{2,0,1:T(8,128)} fusion(f32[128,64,128]{2,0,1:T(8,128)} %scatter_fusion, s32[64]{0:T(128)S(1)} %get-tuple-element.8, f32[64,128,128]{2,1,0:T(8,128)} %fusion.25), kind=kCustom, calls=%fused_computation.7 | custom fusion | flops 1048576 | bytes 12583168 | tf_op jit(solution)/shard_map/scatter-add | solution.py:54
  271.1 13.6 %scatter_fusion.2 = f32[128,64,128]{2,0,1:T(8,128)} fusion(f32[128,64,128]{2,0,1:T(8,128)} %scatter_fusion.1, s32[64]{0:T(128)S(1)} %get-tuple-element.9, f32[64,128,128]{2,1,0:T(8,128)} %fusion.26), kind=kCustom, calls=%fused_computation.8 | custom fusion | flops 1048576 | bytes 12583168 | tf_op jit(solution)/shard_map/scatter-add | solution.py:54
  284.8 13.6 %scatter_fusion.3 = f32[128,64,128]{2,0,1:T(8,128)} fusion(f32[128,64,128]{2,0,1:T(8,128)} %scatter_fusion.2, s32[64]{0:T(128)S(1)} %get-tuple-element.10, f32[64,128,128]{2,1,0:T(8,128)} %fusion.27), kind=kCustom, calls=%fused_computation.9 | custom fusion | flops 1048576 | bytes 12583168 | tf_op jit(solution)/shard_map/scatter-add | solution.py:54
  298.4 13.7 %scatter_fusion.4 = f32[128,64,128]{2,0,1:T(8,128)} fusion(f32[128,64,128]{2,0,1:T(8,128)} %scatter_fusion.3, s32[64]{0:T(128)S(1)} %get-tuple-element.11, f32[64,128,128]{2,1,0:T(8,128)} %fusion.28), kind=kCustom, calls=%fused_computation.10 | custom fusion | flops 1048576 | bytes 12583168 | tf_op jit(solution)/shard_map/scatter-add | solution.py:54
  312.1 13.7 %scatter_fusion.5 = f32[128,64,128]{2,0,1:T(8,128)} fusion(f32[128,64,128]{2,0,1:T(8,128)} %scatter_fusion.4, s32[64]{0:T(128)S(1)} %get-tuple-element.6, f32[64,128,128]{2,1,0:T(8,128)} %fusion.29), kind=kCustom, calls=%fused_computation.11 | custom fusion | flops 1048576 | bytes 12583168 | tf_op jit(solution)/shard_map/scatter-add | solution.py:54
  325.8 4.7 %broadcast_multiply_fusion = f32[128,64,128]{2,0,1:T(8,128)} fusion(f32[128,64,128]{2,0,1:T(8,128)} %scatter_fusion.5), kind=kLoop, calls=%fused_computation.39 | loop fusion | flops 1048576 | bytes 8388608 | tf_op jit(solution)/shard_map/mul | solution.py:82
  330.5 5.6 %copy.42 = f32[128,64,128]{0,2,1:T(8,128)} copy(f32[128,64,128]{2,0,1:T(8,128)} %broadcast_multiply_fusion) | data formatting | bytes 8388608 | tf_op jit(solution)/shard_map/mul | solution.py:82
  336.1 5.2 %fusion = bf16[128,8192]{0,1:T(8,128)(2,1)} fusion(f32[128,64,128]{0,2,1:T(8,128)} %copy.42, f32[128,8192]{0,1:T(8,128)} %all-reduce.2.cloned.1.call-done, f32[]{:T(128)S(6)} %mul_shard_map.3), kind=kLoop, calls=%fused_computation.13 | loop fusion | flops 3145728 | bytes 10485764 | tf_op jit(solution)/shard_map/convert_element_type | solution.py:82
  341.4 2.9 copy.43
  344.3 29.1 %all_to_all.5 = bf16[4,32,8192]{2,1,0:T(8,128)(2,1)S(1)} all-to-all(bf16[4,32,8192]{2,1,0:T(8,128)(2,1)S(1)} %bitcast.99), channel_id=1, replica_groups=mesh['gx'=16,'gy'=4,'gz'=4] {'gy'}, dimensions={0} | all-to-all | bytes 4194304 | tf_op jit(solution)/shard_map/all_to_all | solution.py:21
  373.4 1.3 convert_reduce_fusion
  (34 shorter events, 0.1 us)
Async XLA Ops:
  6.5 10.8 %slice-start.3 = ((bf16[1,4,1,6,128,128]{5,4,3,2,1,0:T(8,128)(2,1)}), bf16[1,1,1,6,128,128]{5,4,3,2,1,0:T(8,128)(2,1)S(1)}, s32[]{:S(2)}) async-start(bf16[1,4,1,6,128,128]{5,4,3,2,1,0:T(8,128)(2,1)} %param.4), calls=%async_computation.6 | async-start | bytes 393216 | tf_op jit(solution)/shard_map/slice | solution.py:64
  6.5 2.2 slice-start.4
  6.5 82.6 %all-gather.6.cloned.1.call-start = ((), (), s32[]{:S(2)}) async-start(), calls=%async_computation.2 | async-start | bytes 13369344 | tf_op jit(solution)/shard_map/all_gather | solution.py:71
  8.7 209.6 %all-reduce.2.cloned.1.call-start = ((), (), s32[]{:S(2)}) async-start(), calls=%async_computation.1 | async-start | bytes 8388608 | tf_op jit(solution)/shard_map/psum | solution.py:76
  30.6 1.4 copy-start.5
  89.2 12.2 %copy-start = (bf16[1,64,1,6,128,128]{5,4,1,3,2,0:T(8,128)(2,1)S(1)}, bf16[1,64,1,6,128,128]{5,4,1,3,2,0:T(8,128)(2,1)}, u32[]{:S(2)}) copy-start(bf16[1,64,1,6,128,128]{5,4,1,3,2,0:T(8,128)(2,1)} %all-gather.6.cloned.1.call-done) | copy-start | bytes 37748740
  95.3 6.0 %copy-start.1 = (bf16[64,128,128]{2,1,0:T(8,128)(2,1)S(1)}, bf16[64,128,128]{2,1,0:T(8,128)(2,1)}, u32[]{:S(2)}) copy-start(bf16[64,128,128]{2,1,0:T(8,128)(2,1)} %gather_fusion.3) | copy-start | bytes 6291460
  101.3 3.6 copy-start.2
  105.0 3.6 copy-start.3
  108.6 3.6 copy-start.4
  218.4 11.7 %slice-start = ((s8[12582912]{0:T(1024)(128)(4,1)}), s8[4194304]{0:T(1024)(128)(4,1)S(1)}, s32[]{:S(2)}) async-start(s8[12582912]{0:T(1024)(128)(4,1)} %bitcast.92), calls=%async_computation.3 | async-start | bytes 8388608
  220.9 9.2 %slice-start.1 = ((s8[12582912]{0:T(1024)(128)(4,1)}), s8[4194304]{0:T(1024)(128)(4,1)S(1)}, s32[]{:S(2)}) async-start(s8[12582912]{0:T(1024)(128)(4,1)} %bitcast.92), calls=%async_computation.4 | async-start | bytes 8388608
  225.5 4.6 %slice-start.2 = ((s8[12582912]{0:T(1024)(128)(4,1)}), s8[4194304]{0:T(1024)(128)(4,1)S(1)}, s32[]{:S(2)}) async-start(s8[12582912]{0:T(1024)(128)(4,1)} %bitcast.92), calls=%async_computation.5 | async-start | bytes 8388608
Sparse Core Ops, SparseCore 0:
  9.2 79.9 all-gather.5
  122.5 95.8 all-reduce.1
where the time goes:
time: 383 us; the launch traced here: 381 us
  waiting for transfers between devices  116 us (30%)
  other arithmetic  96.3 us (25%)
  blocking collectives  74.2 us (19%)
  matrix products  54.3 us (14%)
  local copies, waits for them, and re-layouts  27.4 us (7%)
  between operations  13.5 us (4%)
    psum x1, waiting for transfers between devices, local(): square = lax.psum(partial_square, 'gz')  96 us
    scatter-add x6, other arithmetic, product_two(): summed = summed.at[:, panel_columns[:, column_slot], :].add(product)  82 us
    dot_general x6, matrix products, product_one(): jnp.einsum('rix,iyx->riy', picked, panel_tiles[:, column_slot], preferred...  33.1 us
    all_to_all x1, blocking collectives, sent_and_summed(): lax.all_to_all(tiles, axis, split_axis=0, concat_axis=0, tiled=True)  29.1 us
    all_gather x1, blocking collectives, local(): lax.all_gather(columns_here, 'gx', axis=0, tiled=True)  24.1 us
    all_gather x2, blocking collectives, picked_2(): lax.all_gather(x, axis)  20.9 us
    dot_general x6, matrix products, product_two(): jnp.einsum('rix,ixy->riy', rounded, panel_tiles[:, column_slot], preferre...  20.4 us
    all_gather x1, waiting for transfers between devices, local(): lax.all_gather(tiles_here, 'gx', axis=0, tiled=True)  19.7 us
  transfers between devices with their start and end apart: 2, of which 2 were waited for; matrix products, arithmetic and copies ran while one was open for 4% of the time, Pallas kernels for 0%

commit v1 on v0

v1 whole, which is shorter than its diff:
```python
import functools

import jax
import jax.numpy as jnp
from jax import lax
from jax.experimental import pallas as pl
from jax.experimental.pallas import tpu as pltpu
from jax.sharding import PartitionSpec as P

MESH = pl.DeviceIdType.MESH
F32, BF16 = jnp.float32, jnp.bfloat16
NZ, NX, NY = 8, 4, 4
RB, KP, T = 4, 6, 128
Q = T // NX
ROWS = NZ * Q
HALF = ROWS // 2
UNITS = ((0, 0), (0, 1), (1, 0), (2, 1), (1, 1), (2, 0), (3, 0), (3, 1))


def where_am_i():
    g = lax.axis_index("gx")
    return g // 2, lax.rem(g, 2), lax.axis_index("gy"), lax.axis_index("gz")


def at_z(z, c):
    return {"gx": lax.rem(z + 2 * NZ, NZ) * 2 + c}


def greet(devices):
    barrier = pltpu.get_barrier_semaphore()
    for device in devices:
        pl.semaphore_signal(barrier, inc=1, device_id=device, device_id_type=MESH)
    pl.semaphore_wait(barrier, len(devices))


def nt_dot(a, b):
    return lax.dot_general(a, b, (((1,), (1,)), ((), ())), preferred_element_type=F32)


def front(v_ref, c_ref, p_out, s_out, cp_out,
          pall, lq, cw, cp, mapv, maps, cps, sp, sb, relay, parts, fwd, sfin,
          xs, xr, ds, dr, cs, cr, ls, lr, ws, wr, ys, yr, loc, outs):
    z, c, x, y = where_am_i()
    sib = 1 - c
    xright, xleft, xopp = lax.rem(x + 1, NX), lax.rem(x + 3, NX), lax.rem(x + 2, NX)
    yright, yleft, yopp = lax.rem(y + 1, NY), lax.rem(y + 3, NY), lax.rem(y + 2, NY)
    me2 = {"gx": z * 2 + sib}

    def remote(src, dst, ssem, rsem, device):
        return pltpu.make_async_remote_copy(
            src_ref=src, dst_ref=dst, send_sem=ssem, recv_sem=rsem,
            device_id=device, device_id_type=MESH)

    col_peers = []
    for dx in range(NX):
        for dc in range(2):
            if dx or dc:
                col_peers.append((dx, dc, {"gx": z * 2 + lax.rem(c + dc, 2), "gy": lax.rem(x + dx, NX)}))
    greet([p[2] for p in col_peers] + [at_z(z + d, c) for d in range(1, NZ)]
          + [{"gz": yright}, {"gz": yleft}])

    started = []

    def go(copy):
        copy.start()
        started.append(copy)
        return copy

    def left_copy(dx):
        return remote(v_ref.at[0, :, pl.ds(dx * Q, Q), :], lq.at[z, 0:KP], ls.at[dx], lr.at[0], {"gy": dx})

    def leftc_copy(dx):
        return remote(c_ref, cw.at[z], ls.at[NX + dx], lr.at[1], {"gy": dx})

    @pl.when(x == 0)
    def _():
        for dx in range(1, NX):
            left_copy(dx).start()
            leftc_copy(dx).start()

    xsend = {}
    for order in range(2):
        for way, half, dev in ((0, order, xright), (1, 1 - order, xleft)):
            rows = pl.ds(2 * half, 2)
            xsend[way, half] = go(remote(v_ref.at[rows], pall.at[1 + way, c, rows],
                                         xs.at[way, half], xr.at[way, half], {"gy": dev}))
    dsend = {}
    for half in range(2):
        rows = pl.ds(2 * half, 2)
        dsend[0, half] = go(remote(v_ref.at[rows], pall.at[0, c, rows], ds.at[0, half], dr.at[0, half], me2))
    csend = []
    for n, (dx, dc, dev) in enumerate(col_peers):
        rel = {0: 0, 1: 1, 2: 3, 3: 2}[dx]
        csend.append(go(remote(c_ref, cp.at[rel, c], cs.at[n], cr.at[n], dev)))
    cp[0, c] = c_ref[...]
    for r in range(RB):
        pall[0, c, r] = v_ref[r]
    for zz in range(NZ):
        lq[zz, KP] = jnp.zeros((Q, T), BF16)

    @pl.when(x == 0)
    def _():
        lq[z, 0:KP] = v_ref[0, :, 0:Q, :]
        cw[z] = c_ref[...]
        for dx in range(1, NX):
            left_copy(dx).wait_send()
            leftc_copy(dx).wait_send()

    @pl.when(x != 0)
    def _():
        left_copy(0).wait_recv()
        leftc_copy(0).wait_recv()

    wsend = []
    for d in range(1, NZ):
        wsend.append(go(remote(lq.at[z, 0:KP], lq.at[z, 0:KP], ws.at[0, d], wr.at[0, d], at_z(z + d, c))))
        wsend.append(go(remote(cw.at[z], cw.at[z], ws.at[1, d], wr.at[1, d], at_z(z + d, c))))
    for copy in csend:
        copy.wait_recv()
    to_smem = pltpu.make_async_copy(cp, cps, loc.at[0])
    to_smem.start()
    for copy in wsend:
        copy.wait_recv()
    lane = lax.broadcasted_iota(jnp.int32, (1, T), 1)
    for zz in range(NZ):
        row = cw[zz]
        found = jnp.full((1, T), KP, jnp.int32)
        for k in range(KP):
            found = jnp.where(jnp.broadcast_to(row[:, k : k + 1], (1, T)) == lane, k, found)
        mapv[zz] = found
    map_copy = pltpu.make_async_copy(mapv, maps, loc.at[1])
    map_copy.start()
    to_smem.wait()
    map_copy.wait()
    cols_out = pltpu.make_async_copy(cp, cp_out, outs.at[0])
    cols_out.start()

    def square_part(rel, half):
        u = rel * 2 + half

        def body(n, carry):
            block, r = n // 2, lax.rem(n, 2)
            row = 2 * half + r
            wide = []
            for k in range(KP):
                col = cps[rel, block, 0, row * KP + k]
                wide.append(jnp.concatenate([lq[zz, maps[zz, 0, col]] for zz in range(NZ)], axis=0))
            total = None
            for k in range(0, KP, 2):
                lhs = jnp.concatenate(wide[k : k + 2], axis=1)
                rhs = jnp.concatenate([pall[rel, block, row, k], pall[rel, block, row, k + 1]], axis=1)
                prod = nt_dot(lhs, rhs)
                total = prod if total is None else total + prod
            sp[u, n] = total
            sb[u, n] = total.astype(BF16)
            return carry

        lax.fori_loop(0, 4, body, 0)

    top, bottom = pl.ds(0, HALF), pl.ds(HALF, HALF)
    R, L = {"gz": yright}, {"gz": yleft}

    def ycopy(u, m, src, dst, dev):
        return remote(src, dst, ys.at[u, m], yr.at[u, m], dev)

    def message(u, m):
        if m == 0:
            return ycopy(u, 0, sb.at[u, yopp, bottom], relay.at[u, 0], R)
        if m == 1:
            return ycopy(u, 1, sb.at[u, yopp, top], relay.at[u, 1], L)
        if m == 2:
            return ycopy(u, 2, sb.at[u, yright, top], parts.at[u, 0], R)
        if m == 3:
            return ycopy(u, 3, sb.at[u, yleft, bottom], parts.at[u, 1], L)
        if m == 4:
            return ycopy(u, 4, fwd.at[u, 0], parts.at[u, 2], R)
        if m == 5:
            return ycopy(u, 5, fwd.at[u, 1], parts.at[u, 3], L)
        if m in (6, 7):
            rows = top if m == 6 else bottom
            return ycopy(u, m, sfin.at[u, y, rows], sfin.at[u, y, rows], R)
        if m in (8, 9):
            rows = top if m == 8 else bottom
            return ycopy(u, m, sfin.at[u, y, rows], sfin.at[u, y, rows], L)
        if m == 10:
            return ycopy(u, 10, sfin.at[u, yleft, top], sfin.at[u, yleft, top], R)
        return ycopy(u, 11, sfin.at[u, yright, bottom], sfin.at[u, yright, bottom], L)

    def send_parts(u):
        for m in range(4):
            go(message(u, m))

    def send_relay(u):
        message(u, 0).wait_recv()
        fwd[u, 0] = (sp[u, yright, HALF:ROWS] + relay[u, 0].astype(F32)).astype(BF16)
        go(message(u, 4))
        message(u, 1).wait_recv()
        fwd[u, 1] = (sp[u, yleft, 0:HALF] + relay[u, 1].astype(F32)).astype(BF16)
        go(message(u, 5))

    def send_sum(u):
        message(u, 2).wait_recv()
        message(u, 5).wait_recv()
        sfin[u, y, 0:HALF] = (sp[u, y, 0:HALF] + parts[u, 0].astype(F32) + parts[u, 3].astype(F32)).astype(BF16)
        go(message(u, 6))
        go(message(u, 8))
        message(u, 3).wait_recv()
        message(u, 4).wait_recv()
        sfin[u, y, HALF:ROWS] = (sp[u, y, HALF:ROWS] + parts[u, 1].astype(F32) + parts[u, 2].astype(F32)).astype(BF16)
        go(message(u, 9))
        go(message(u, 7))

    def send_forward(u):
        message(u, 6).wait_recv()
        go(message(u, 10))
        message(u, 9).wait_recv()
        go(message(u, 11))

    def finish(u):
        for m in (7, 8, 10, 11):
            message(u, m).wait_recv()
        copy = pltpu.make_async_copy(sfin.at[u], s_out.at[u], outs.at[5 + u])
        copy.start()
        return copy

    final = [cols_out]

    def arrive(rel, half):
        rows = pl.ds(2 * half, 2)
        dsend[rel, half] = go(remote(pall.at[rel, c, rows], pall.at[rel, c, rows],
                                     ds.at[rel, half], dr.at[rel, half], me2))

    def p_done(rel):
        copy = pltpu.make_async_copy(pall.at[rel], p_out.at[rel], outs.at[1 + rel])
        copy.start()
        final.append(copy)

    def u_of(rel, half):
        return rel * 2 + half

    for half in range(2):
        dsend[0, half].wait_recv()
        square_part(0, half)
        send_parts(u_of(0, half))
    p_done(0)
    xsend[0, 0].wait_recv()
    rows = pl.ds(0, 2)
    xsend[2, 0] = go(remote(pall.at[1, c, rows], pall.at[3, c, rows], xs.at[2, 0], xr.at[2, 0], {"gy": xright}))
    arrive(1, 0)
    xsend[1, 1].wait_recv()
    rows = pl.ds(2, 2)
    xsend[2, 1] = go(remote(pall.at[2, c, rows], pall.at[3, c, rows], xs.at[2, 1], xr.at[2, 1], {"gy": xleft}))
    arrive(2, 1)
    for half in range(2):
        send_relay(u_of(0, half))
    for rel, half in ((1, 0), (2, 1)):
        dsend[rel, half].wait_recv()
        square_part(rel, half)
        send_parts(u_of(rel, half))
    for half in range(2):
        send_sum(u_of(0, half))
    for rel, half in ((1, 0), (2, 1)):
        send_relay(u_of(rel, half))
    xsend[0, 1].wait_recv()
    arrive(1, 1)
    xsend[1, 0].wait_recv()
    arrive(2, 0)
    for half in range(2):
        send_forward(u_of(0, half))
    for rel, half in ((1, 1), (2, 0)):
        dsend[rel, half].wait_recv()
        square_part(rel, half)
        send_parts(u_of(rel, half))
    p_done(1)
    p_done(2)
    for rel, half in ((1, 0), (2, 1)):
        send_sum(u_of(rel, half))
    for rel, half in ((1, 1), (2, 0)):
        send_relay(u_of(rel, half))
    xsend[2, 0].wait_recv()
    arrive(3, 0)
    xsend[2, 1].wait_recv()
    arrive(3, 1)
    for rel, half in ((3, 0), (3, 1)):
        dsend[rel, half].wait_recv()
        square_part(rel, half)
        send_parts(u_of(rel, half))
    p_done(3)
    for rel, half in ((1, 0), (2, 1)):
        send_forward(u_of(rel, half))
    for rel, half in ((1, 1), (2, 0)):
        send_sum(u_of(rel, half))
    for half in range(2):
        send_relay(u_of(3, half))
    for half in range(2):
        final.append(finish(u_of(0, half)))
    for rel, half in ((1, 1), (2, 0)):
        send_forward(u_of(rel, half))
    for half in range(2):
        send_sum(u_of(3, half))
    for rel, half in ((1, 0), (2, 1)):
        final.append(finish(u_of(rel, half)))
    for half in range(2):
        send_forward(u_of(3, half))
    for rel, half in ((1, 1), (2, 0), (3, 0), (3, 1)):
        final.append(finish(u_of(rel, half)))
    for copy in started:
        copy.wait_send()
    for copy in final:
        copy.wait()


def middle(cols, p_ref, s_ref, r_ref, acc):
    n = pl.program_id(0)
    rel, block = n // 2, lax.rem(n, 2)
    z, c, x, y = where_am_i()

    @pl.when(n == 0)
    def _():
        acc[...] = jnp.zeros_like(acc)

    slab = lax.rem(x + jnp.where(rel == 0, 0, jnp.where(rel == 1, NX - 1, jnp.where(rel == 2, 1, 2))), NX)

    @pl.when(slab == y)
    def _():
        for r in range(RB):
            mine = s_ref[r // 2, block * 2 + r % 2].astype(F32)
            at = 8 * z + 4 * block + r
            acc[at] += -1.5 * mine

    def body(r, carry):
        mine = s_ref[r // 2, block * 2 + lax.rem(r, 2)]
        for k in range(KP):
            col = cols[rel, block, 0, r * KP + k]
            acc[col] += jnp.dot(mine, p_ref[0, 0, r, k], preferred_element_type=F32)
        return carry

    lax.fori_loop(0, RB, body, 0)

    @pl.when(n == 2 * NX - 1)
    def _():
        def out(j, carry):
            tile = (-2.0 * acc[j]).astype(BF16)
            for zz in range(NZ):
                r_ref[zz, j] = tile[zz * Q : (zz + 1) * Q]
            return carry

        lax.fori_loop(0, 64, out, 0)


SUBS = 8
PER = 64 // SUBS


def back(r_ref, o_ref, rbuf, sbuf, ssem, rsem):
    z, c, x, y = where_am_i()
    devs = (at_z(z + 1, c), at_z(z - 1, c))
    greet(devs)

    def tiles(sub):
        return pl.ds(sub * PER, PER)

    def copy(way, step, sub, src):
        return pltpu.make_async_remote_copy(
            src_ref=src, dst_ref=rbuf.at[way, step, sub],
            send_sem=ssem.at[way, step, sub], recv_sem=rsem.at[way, step, sub],
            device_id=devs[way], device_id_type=MESH)

    started = []
    relays = (range(0, SUBS // 2), range(SUBS // 2, SUBS))
    for step in range(4):
        dest = (lax.rem(z + 4 - step, NZ), lax.rem(z + 4 + step, NZ))
        for pos in range(SUBS):
            for way in range(2):
                sub = pos if way == 0 else (pos + SUBS // 2) % SUBS
                first = sub in relays[way]
                if step == 0 and not first:
                    continue
                own = r_ref.at[dest[way], tiles(sub)]
                if step == 0 or (step == 1 and not first):
                    move = copy(way, step, sub, own)
                else:
                    copy(way, step - 1, sub, own).wait_recv()
                    sbuf[way, step, sub] = (own[...].astype(F32) + rbuf[way, step - 1, sub].astype(F32)).astype(BF16)
                    move = copy(way, step, sub, sbuf.at[way, step, sub])
                move.start()
                started.append(move)
    for sub in range(SUBS):
        for way in range(2):
            copy(way, 3, sub, sbuf.at[way, 3, sub]).wait_recv()
        total = (r_ref[z, tiles(sub)].astype(F32) + rbuf[0, 3, sub].astype(F32) + rbuf[1, 3, sub].astype(F32))
        for t in range(PER):
            j = sub * PER + t
            o_ref[:, j * T : (j + 1) * T] = total[t]
    for move in started:
        move.wait_send()


def local(block_values, block_cols):
    v = block_values[0, :, 0]
    cflat = jnp.pad(block_cols.reshape(1, RB * KP), ((0, 0), (0, T - RB * KP)))
    vmem = pl.BlockSpec(memory_space=pltpu.VMEM)
    anys = pl.BlockSpec(memory_space=pl.ANY)
    sem = pltpu.SemaphoreType.DMA
    p_all, s_all, cols = pl.pallas_call(
        front,
        out_shape=(
            jax.ShapeDtypeStruct((NX, 2, RB, KP, T, T), BF16),
            jax.ShapeDtypeStruct((8, 4, ROWS, T), BF16),
            jax.ShapeDtypeStruct((NX, 2, 1, T), jnp.int32),
        ),
        in_specs=[vmem, vmem],
        out_specs=(anys, anys, anys),
        scratch_shapes=[
            pltpu.VMEM((NX, 2, RB, KP, T, T), BF16),
            pltpu.VMEM((NZ, KP + 1, Q, T), BF16),
            pltpu.VMEM((NZ, 1, T), jnp.int32),
            pltpu.VMEM((NX, 2, 1, T), jnp.int32),
            pltpu.VMEM((NZ, 1, T), jnp.int32),
            pltpu.SMEM((NZ, 1, T), jnp.int32),
            pltpu.SMEM((NX, 2, 1, T), jnp.int32),
            pltpu.VMEM((8, 4, ROWS, T), F32),
            pltpu.VMEM((8, 4, ROWS, T), BF16),
            pltpu.VMEM((8, 2, HALF, T), BF16),
            pltpu.VMEM((8, 4, HALF, T), BF16),
            pltpu.VMEM((8, 2, HALF, T), BF16),
            pltpu.VMEM((8, 4, ROWS, T), BF16),
            sem((3, 2)), sem((3, 2)), sem((4, 2)), sem((4, 2)),
            sem((7,)), sem((7,)), sem((8,)), sem((2,)),
            sem((2, NZ)), sem((2, NZ)), sem((8, 12)), sem((8, 12)),
            sem((2,)), sem((13,)),
        ],
        compiler_params=pltpu.CompilerParams(
            collective_id=0, has_side_effects=True, vmem_limit_bytes=40 << 20),
        name="front",
    )(v, cflat)
    r_all = pl.pallas_call(
        middle,
        out_shape=jax.ShapeDtypeStruct((NZ, 64, Q, T), BF16),
        grid=(8,),
        in_specs=[
            pl.BlockSpec(memory_space=pltpu.SMEM),
            pl.BlockSpec((1, 1, RB, KP, T, T), lambda n: (n // 2, n % 2, 0, 0, 0, 0)),
            pl.BlockSpec((2, 4, ROWS, T), lambda n: (n // 2, 0, 0, 0)),
        ],
        out_specs=vmem,
        scratch_shapes=[pltpu.VMEM((64, ROWS, T), F32)],
        compiler_params=pltpu.CompilerParams(
            dimension_semantics=("arbitrary",), vmem_limit_bytes=40 << 20),
        name="middle",
    )(cols, p_all, s_all)
    return pl.pallas_call(
        back,
        out_shape=jax.ShapeDtypeStruct((Q, 64 * T), F32),
        in_specs=[vmem],
        out_specs=vmem,
        scratch_shapes=[
            pltpu.VMEM((2, 4, SUBS, PER, Q, T), BF16),
            pltpu.VMEM((2, 4, SUBS, PER, Q, T), BF16),
            sem((2, 4, SUBS)), sem((2, 4, SUBS)),
        ],
        compiler_params=pltpu.CompilerParams(
            collective_id=1, has_side_effects=True, vmem_limit_bytes=40 << 20),
        name="back",
    )(r_all)


def solution(mesh):
    in_specs = (P("gy", "gx", "gz", None, None, None), P("gy", "gx", "gz", None))
    return jax.shard_map(local, mesh=mesh, in_specs=in_specs, out_specs=P(("gx", "gy"), "gz"), check_vma=False)
```

time: 383 us -> 134 us (0.35)
  Pallas kernels: 0 us -> 130 us
  waiting for transfers between devices: 116 us -> 0 us
  other arithmetic: 96.3 us -> 1.34 us
  blocking collectives: 74.2 us -> 0 us
  matrix products: 54.3 us -> 0 us
  local copies, waits for them, and re-layouts: 27.4 us -> 2.71 us
  between operations: 13.5 us -> 0.03 us
    pallas_call x0 -> x3, Pallas kernels: none -> 130 us  [the longest x1 75 us: local(): pl.pallas_call(front, out_shape=(jax.ShapeDtypeStruct((NX, 2, RB, KP, T,...]
    psum x1 -> x0, waiting for transfers between devices: 96 us -> none  [local(): square = lax.psum(partial_square, 'gz')]
    scatter-add x6 -> x0, other arithmetic: 82 us -> none  [product_two(): summed = summed.at[:, panel_columns[:, column_slot], :].add(product)]
    dot_general x13 -> x0, matrix products: 54.3 us -> none  [the longest x6 33.1 us: product_one(): jnp.einsum('rix,iyx->riy', picked, panel_tiles[:, column_slot], preferred...]
    all_gather x3 -> x0, blocking collectives: 45.1 us -> none  [the longest x1 24.1 us: local(): lax.all_gather(columns_here, 'gx', axis=0, tiled=True)]
    all_to_all x1 -> x0, blocking collectives: 29.1 us -> none  [sent_and_summed(): lax.all_to_all(tiles, axis, split_axis=0, concat_axis=0, tiled=True)]
    all_gather x1 -> x0, waiting for transfers between devices: 19.7 us -> none  [local(): lax.all_gather(tiles_here, 'gx', axis=0, tiled=True)]
    gather x6 -> x0, local copies, waits for them, and re-layouts: 12.9 us -> none  [product_one(): picked = jnp.take(left_panel, panel_columns[:, column_slot], axis=1)]
  transfers between devices with their start and end apart: 2 -> 0, of which waited for: 2 -> 0; matrix products, arithmetic and copies ran while one was open for 4% -> 0% of each run, Pallas kernels for 0% -> 0%
where the time goes in v1:
time: 134 us
  Pallas kernels  130 us (97%)
  local copies, waits for them, and re-layouts  2.71 us (2%)
  other arithmetic  1.34 us (1%)
    pallas_call x1, Pallas kernels, local(): pl.pallas_call(front, out_shape=(jax.ShapeDtypeStruct((NX, 2, RB, KP, T,...  75 us
    pallas_call x1, Pallas kernels, local(): pl.pallas_call(back, out_shape=jax.ShapeDtypeStruct((Q, 64 * T), F32), in...  44.1 us
    pallas_call x1, Pallas kernels, local(): pl.pallas_call(middle, out_shape=jax.ShapeDtypeStruct((NZ, 64, Q, T), BF1...  10.8 us

profile of v1, /device:TPU:1, one launch (start us, length us, event | category | flops | bytes accessed | tf_op | source)
XLA Modules:
  0.0 134.0 jit_solution(17766215095252748138)
XLA Ops:
  0.0 0.5 broadcast.5
  0.5 1.3 %reduce.3 = s32[4,6]{1,0:T(4,128)S(1)} reduce(s32[1,4,1,6]{3,2,1,0:T(1,128)} %param.3, s32[]{:T(128)} %broadcast.5), dimensions={0,2}, to_apply=%param.3.reduce_sub_computation.3 | reduce | bytes 196 | tf_op args[1]
  1.9 0.1 reshape.3
  2.0 0.0 copy-start
  2.0 1.1 copy-done
  3.1 75.0 %front.1 = (bf16[4,2,4,6,128,128]{5,4,3,2,1,0:T(8,128)(2,1)S(1)}, bf16[8,4,256,128]{3,2,1,0:T(8,128)(2,1)S(1)}, s32[4,2,1,128]{3,2,1,0:T(1,128)S(1)}) custom-call(bf16[4,6,128,128]{3,2,1,0:T(8,128)(2,1)S(1)} %bitcast.1, s32[1,128]{1,0:T(1,128)S(1)} %pad.4.c_ref), custom_call_target="tpu_custom_call" | custom-call | tf_op jit(solution)/shard_map/front/pallas_call | solution.py:405
  78.1 10.8 %middle.1.r_ref = bf16[8,64,32,128]{3,2,1,0:T(8,128)(2,1)S(1)} custom-call(s32[4,2,1,128]{3,2,1,0:T(1,128)S(1)} %get-tuple-element.8.cols, bf16[4,2,4,6,128,128]{5,4,3,2,1,0:T(8,128)(2,1)S(1)} %get-tuple-element.9.p_ref, bf16[8,4,256,128]{3,2,1,0:T(8,128)(2,1)S(1)} %get-tuple-element.10.s_ref), custom_call_target="tpu_custom_call" | custom-call | tf_op jit(solution)/shard_map/middle/pallas_call | solution.py:437
  88.9 44.1 %back.1 = f32[32,8192]{1,0:T(8,128)S(1)} custom-call(bf16[8,64,32,128]{3,2,1,0:T(8,128)(2,1)S(1)} %middle.1.r_ref), custom_call_target="tpu_custom_call" | custom-call | tf_op jit(solution)/shard_map/back/pallas_call | solution.py:452
  133.0 1.0 copy.4
  (1 shorter events, 0.0 us)
Async XLA Ops:
  2.0 1.1 copy-start

commit v2 on v1

--- a/solution.py
+++ b/solution.py
@@ -14,6 +14,9 @@
 Q = T // NX
 ROWS = NZ * Q
 HALF = ROWS // 2
+TILES = NX * 2 * RB * KP
+SUBS = 8
+PER = 64 // SUBS
 UNITS = ((0, 0), (0, 1), (1, 0), (2, 1), (1, 1), (2, 0), (3, 0), (3, 1))
 
 
@@ -37,9 +40,43 @@
     return lax.dot_general(a, b, (((1,), (1,)), ((), ())), preferred_element_type=F32)
 
 
-def front(v_ref, c_ref, p_out, s_out, cp_out,
-          pall, lq, cw, cp, mapv, maps, cps, sp, sb, relay, parts, fwd, sfin,
-          xs, xr, ds, dr, cs, cr, ls, lr, ws, wr, ys, yr, loc, outs):
+def sort_tiles(cp, colv, prev, ordv):
+    for n in range(2 * NX * RB):
+        colv[n : n + 1, :] = cp[n // 8, n // 4 % 2, n % 4]
+    count = 2 * NX * RB
+    cols = colv[...]
+    lanes = lax.broadcasted_iota(jnp.int32, (count, T), 1)
+    hits = [jnp.broadcast_to(cols[:, k : k + 1], (count, T)) == lanes for k in range(KP)]
+    listed = jnp.zeros((count, T), jnp.int32)
+    for hit in hits:
+        listed = listed + jnp.where(hit, 1, 0)
+    run = jnp.zeros((1, T), jnp.int32)
+    for n in range(count):
+        prev[n : n + 1, :] = run
+        run = run + listed[n : n + 1, :]
+    lane = lax.broadcasted_iota(jnp.int32, (1, T), 1)
+    upto = run
+    for shift in (1, 2, 4, 8, 16, 32, 64):
+        upto = upto + jnp.where(lane >= shift, pltpu.roll(upto, shift, 1), 0)
+    before = prev[...]
+    place = (jnp.broadcast_to(upto - run, (count, T)) + before) * 2 + jnp.where(before > 0, 1, 0)
+    ordv[2] = jnp.where(run > 0, upto - 1, TILES)
+    tile = lax.broadcasted_iota(jnp.int32, (count, T), 0) * KP
+    picked = [jnp.zeros((count, T), jnp.int32) for part in range(2)]
+    for k, hit in enumerate(hits):
+        mine = jnp.sum(jnp.where(hit, place, 0), axis=1, keepdims=True)
+        mine = jnp.broadcast_to(mine, (count, T))
+        code = (tile + k) * 2 + jnp.where(lax.rem(mine, 2) == 1, 1, 0)
+        for part in range(2):
+            picked[part] = jnp.where(mine // 2 == lanes + part * T, code, picked[part])
+    for part in range(2):
+        ordv[part] = jnp.sum(picked[part], axis=0, keepdims=True)
+
+
+def step(v_hbm, c_in, o_ref,
+         v_ref, c_ref, pall, lq, cw, cp, mapv, maps, cps, sp, sb, relay, parts, fwd, sfin,
+         colv, prev, ordv, ords, prods, sums, rbuf, sbuf,
+         xs, xr, ds, dr, cs, cr, ls, lr, ws, wr, ys, yr, loc, zs, zr):
     z, c, x, y = where_am_i()
     sib = 1 - c
     xright, xleft, xopp = lax.rem(x + 1, NX), lax.rem(x + 3, NX), lax.rem(x + 2, NX)
@@ -50,6 +87,12 @@
         return pltpu.make_async_remote_copy(
             src_ref=src, dst_ref=dst, send_sem=ssem, recv_sem=rsem,
             device_id=device, device_id_type=MESH)
+
+    fetch = pltpu.make_async_copy(v_hbm, v_ref, loc.at[2])
+    fetch.start()
+    for r in range(RB):
+        c_ref[r] = jnp.zeros((1, T), jnp.int32)
+        c_ref[r, :, 0:KP] = c_in[0, r]
 
     col_peers = []
     for dx in range(NX):
@@ -59,6 +102,7 @@
     greet([p[2] for p in col_peers] + [at_z(z + d, c) for d in range(1, NZ)]
           + [{"gz": yright}, {"gz": yleft}])
 
+    fetch.wait()
     started = []
 
     def go(copy):
@@ -70,7 +114,7 @@
         return remote(v_ref.at[0, :, pl.ds(dx * Q, Q), :], lq.at[z, 0:KP], ls.at[dx], lr.at[0], {"gy": dx})
 
     def leftc_copy(dx):
-        return remote(c_ref, cw.at[z], ls.at[NX + dx], lr.at[1], {"gy": dx})
+        return remote(c_ref.at[0], cw.at[z], ls.at[NX + dx], lr.at[1], {"gy": dx})
 
     @pl.when(x == 0)
     def _():
@@ -101,7 +145,7 @@
     @pl.when(x == 0)
     def _():
         lq[z, 0:KP] = v_ref[0, :, 0:Q, :]
-        cw[z] = c_ref[...]
+        cw[z] = c_ref[0]
         for dx in range(1, NX):
             left_copy(dx).wait_send()
             leftc_copy(dx).wait_send()
@@ -132,8 +176,6 @@
     map_copy.start()
     to_smem.wait()
     map_copy.wait()
-    cols_out = pltpu.make_async_copy(cp, cp_out, outs.at[0])
-    cols_out.start()
 
     def square_part(rel, half):
         u = rel * 2 + half
@@ -143,7 +185,7 @@
             row = 2 * half + r
             wide = []
             for k in range(KP):
-                col = cps[rel, block, 0, row * KP + k]
+                col = cps[rel, block, row, 0, k]
                 wide.append(jnp.concatenate([lq[zz, maps[zz, 0, col]] for zz in range(NZ)], axis=0))
             total = None
             for k in range(0, KP, 2):
@@ -219,21 +261,27 @@
     def finish(u):
         for m in (7, 8, 10, 11):
             message(u, m).wait_recv()
-        copy = pltpu.make_async_copy(sfin.at[u], s_out.at[u], outs.at[5 + u])
-        copy.start()
-        return copy
-
-    final = [cols_out]
+
 
     def arrive(rel, half):
         rows = pl.ds(2 * half, 2)
         dsend[rel, half] = go(remote(pall.at[rel, c, rows], pall.at[rel, c, rows],
                                      ds.at[rel, half], dr.at[rel, half], me2))
 
-    def p_done(rel):
-        copy = pltpu.make_async_copy(pall.at[rel], p_out.at[rel], outs.at[1 + rel])
-        copy.start()
-        final.append(copy)
+    def products(rel, half):
+        u = rel * 2 + half
+
+        def body(n, carry):
+            block, r = n // 2, lax.rem(n, 2)
+            row = 2 * half + r
+            wide = jnp.concatenate([pall[rel, block, row, k] for k in range(KP)], axis=1)
+            both = jnp.dot(sfin[u, n], wide, preferred_element_type=F32)
+            at = ((rel * 2 + block) * RB + row) * KP
+            for k in range(KP):
+                prods[at + k] = both[:, k * T : (k + 1) * T]
+            return carry
+
+        lax.fori_loop(0, 4, body, 0)
 
     def u_of(rel, half):
         return rel * 2 + half
@@ -242,7 +290,9 @@
         dsend[0, half].wait_recv()
         square_part(0, half)
         send_parts(u_of(0, half))
-    p_done(0)
+    sort_tiles(cp, colv, prev, ordv)
+    order_copy = pltpu.make_async_copy(ordv, ords, loc.at[0])
+    order_copy.start()
     xsend[0, 0].wait_recv()
     rows = pl.ds(0, 2)
     xsend[2, 0] = go(remote(pall.at[1, c, rows], pall.at[3, c, rows], xs.at[2, 0], xr.at[2, 0], {"gy": xright}))
@@ -271,43 +321,141 @@
         dsend[rel, half].wait_recv()
         square_part(rel, half)
         send_parts(u_of(rel, half))
-    p_done(1)
-    p_done(2)
     for rel, half in ((1, 0), (2, 1)):
         send_sum(u_of(rel, half))
     for rel, half in ((1, 1), (2, 0)):
         send_relay(u_of(rel, half))
+    for rel, half in ((1, 0), (2, 1)):
+        send_forward(u_of(rel, half))
+    for rel, half in ((1, 1), (2, 0)):
+        send_sum(u_of(rel, half))
     xsend[2, 0].wait_recv()
     arrive(3, 0)
     xsend[2, 1].wait_recv()
     arrive(3, 1)
+    for half in range(2):
+        finish(u_of(0, half))
+        products(0, half)
     for rel, half in ((3, 0), (3, 1)):
         dsend[rel, half].wait_recv()
         square_part(rel, half)
         send_parts(u_of(rel, half))
-    p_done(3)
-    for rel, half in ((1, 0), (2, 1)):
-        send_forward(u_of(rel, half))
-    for rel, half in ((1, 1), (2, 0)):
-        send_sum(u_of(rel, half))
-    for half in range(2):
-        send_relay(u_of(3, half))
-    for half in range(2):
-        final.append(finish(u_of(0, half)))
     for rel, half in ((1, 1), (2, 0)):
         send_forward(u_of(rel, half))
+    for rel, half in ((1, 0), (2, 1)):
+        finish(u_of(rel, half))
+        products(rel, half)
+    for half in range(2):
+        send_relay(u_of(3, half))
     for half in range(2):
         send_sum(u_of(3, half))
-    for rel, half in ((1, 0), (2, 1)):
-        final.append(finish(u_of(rel, half)))
     for half in range(2):
         send_forward(u_of(3, half))
     for rel, half in ((1, 1), (2, 0), (3, 0), (3, 1)):
-        final.append(finish(u_of(rel, half)))
+        finish(u_of(rel, half))
+        products(rel, half)
+    order_copy.wait()
+    zdevs = (at_z(z + 1, c), at_z(z - 1, c))
+    ahead = lax.rem(y - x + NX, NX)
+    here = jnp.where(ahead == 0, 0, jnp.where(ahead == 3, 1, jnp.where(ahead == 1, 2, 3)))
+
+    def rows_of(dest):
+        return pl.ds(pl.multiple_of(dest * Q, Q), Q)
+
+    def scan(way, dest):
+        rows = rows_of(dest)
+        run = jnp.zeros((Q, T), F32)
+        for part in range(2):
+            def body(n, run, part=part):
+                for m in range(8):
+                    t = n * 8 + m
+                    code = ords[part, 0, t]
+                    tile = prods[code // 2, rows]
+                    run = tile + run * lax.rem(code, 2).astype(F32)
+                    sums[way, part * T + t] = run
+                return run
+
+            run = lax.fori_loop(0, 16 if part == 0 else TILES // 8 - 16, body, run)
+        for n in range(2 * RB):
+            last = ords[2, 0, 8 * z + n]
+            mine = sfin[here * 2 + n % 4 // 2, n // 4 * 2 + n % 2, rows].astype(F32)
+            sums[way, TILES + 1 + n] = sums[way, last] - 1.5 * mine
+
+    def result_tile(way, j):
+        own = j - 8 * z
+        inside = jnp.logical_and(own >= 0, own < 8)
+        return -2.0 * sums[way, jnp.where(inside, TILES + 1 + own, ords[2, 0, j])]
+
+    def zcopy(way, hop, sub):
+        return pltpu.make_async_remote_copy(
+            src_ref=sbuf.at[way, hop, sub], dst_ref=rbuf.at[way, hop, sub],
+            send_sem=zs.at[way, hop, sub], recv_sem=zr.at[way, hop, sub],
+            device_id=zdevs[way], device_id_type=MESH)
+
+    def emit(way, hop, sub, have):
+        if have:
+            zcopy(way, hop - 1, sub).wait_recv()
+        for t in range(PER):
+            tile = result_tile(0 if hop == 0 else way, sub * PER + t)
+            if have:
+                tile = tile + rbuf[way, hop - 1, sub, t].astype(F32)
+            sbuf[way, hop, sub, t] = tile.astype(BF16)
+        zcopy(way, hop, sub).start()
+
+    for way in range(2):
+        sums[way, TILES] = jnp.zeros((Q, T), F32)
+    hs = SUBS // 2
+    scan(0, lax.rem(z + 4, NZ))
+
+    def hop0(n, carry):
+        emit(0, 0, n, False)
+        emit(1, 0, n + hs, False)
+        return carry
+
+    lax.fori_loop(0, hs, hop0, 0)
+    for hop in range(1, 4):
+        scan(0, lax.rem(z + 4 - hop, NZ))
+        scan(1, lax.rem(z + 4 + hop, NZ))
+
+        def fresh(n, carry, hop=hop):
+            emit(0, hop, n + hs, hop > 1)
+            emit(1, hop, n, hop > 1)
+            return carry
+
+        def relayed(n, carry, hop=hop):
+            emit(0, hop, n, True)
+            emit(1, hop, n + hs, True)
+            return carry
+
+        lax.fori_loop(0, hs, fresh, 0)
+        lax.fori_loop(0, hs, relayed, 0)
+    scan(0, z)
+    for n in range(SUBS):
+        for way in range(2):
+            sub = (n + (hs if way == 0 else 0)) % SUBS
+            zcopy(way, 3, sub).wait_recv()
+    for sub in range(SUBS):
+        for t in range(PER):
+            j = sub * PER + t
+            tile = result_tile(0, j) + rbuf[0, 3, sub, t].astype(F32) + rbuf[1, 3, sub, t].astype(F32)
+            o_ref[:, j * T : (j + 1) * T] = tile
+
+    def drain(n, carry):
+        for way in range(2):
+            for hop in range(1, 4):
+                zcopy(way, hop, n).wait_send()
+        return carry
+
+    lax.fori_loop(0, SUBS, drain, 0)
+
+    def drain0(n, carry):
+        zcopy(0, 0, n).wait_send()
+        zcopy(1, 0, n + hs).wait_send()
+        return carry
+
+    lax.fori_loop(0, hs, drain0, 0)
     for copy in started:
         copy.wait_send()
-    for copy in final:
-        copy.wait()
 
 
 def middle(cols, p_ref, s_ref, r_ref, acc):
@@ -331,7 +479,7 @@
     def body(r, carry):
         mine = s_ref[r // 2, block * 2 + lax.rem(r, 2)]
         for k in range(KP):
-            col = cols[rel, block, 0, r * KP + k]
+            col = cols[rel, block, r, 0, k]
             acc[col] += jnp.dot(mine, p_ref[0, 0, r, k], preferred_element_type=F32)
         return carry
 
@@ -348,121 +496,46 @@
         lax.fori_loop(0, 64, out, 0)
 
 
-SUBS = 8
-PER = 64 // SUBS
-
-
-def back(r_ref, o_ref, rbuf, sbuf, ssem, rsem):
-    z, c, x, y = where_am_i()
-    devs = (at_z(z + 1, c), at_z(z - 1, c))
-    greet(devs)
-
-    def tiles(sub):
-        return pl.ds(sub * PER, PER)
-
-    def copy(way, step, sub, src):
-        return pltpu.make_async_remote_copy(
-            src_ref=src, dst_ref=rbuf.at[way, step, sub],
-            send_sem=ssem.at[way, step, sub], recv_sem=rsem.at[way, step, sub],
-            device_id=devs[way], device_id_type=MESH)
-
-    started = []
-    relays = (range(0, SUBS // 2), range(SUBS // 2, SUBS))
-    for step in range(4):
-        dest = (lax.rem(z + 4 - step, NZ), lax.rem(z + 4 + step, NZ))
-        for pos in range(SUBS):
-            for way in range(2):
-                sub = pos if way == 0 else (pos + SUBS // 2) % SUBS
-                first = sub in relays[way]
-                if step == 0 and not first:
-                    continue
-                own = r_ref.at[dest[way], tiles(sub)]
-                if step == 0 or (step == 1 and not first):
-                    move = copy(way, step, sub, own)
-                else:
-                    copy(way, step - 1, sub, own).wait_recv()
-                    sbuf[way, step, sub] = (own[...].astype(F32) + rbuf[way, step - 1, sub].astype(F32)).astype(BF16)
-                    move = copy(way, step, sub, sbuf.at[way, step, sub])
-                move.start()
-                started.append(move)
-    for sub in range(SUBS):
-        for way in range(2):
-            copy(way, 3, sub, sbuf.at[way, 3, sub]).wait_recv()
-        total = (r_ref[z, tiles(sub)].astype(F32) + rbuf[0, 3, sub].astype(F32) + rbuf[1, 3, sub].astype(F32))
-        for t in range(PER):
-            j = sub * PER + t
-            o_ref[:, j * T : (j + 1) * T] = total[t]
-    for move in started:
-        move.wait_send()
-
-
 def local(block_values, block_cols):
-    v = block_values[0, :, 0]
-    cflat = jnp.pad(block_cols.reshape(1, RB * KP), ((0, 0), (0, T - RB * KP)))
-    vmem = pl.BlockSpec(memory_space=pltpu.VMEM)
-    anys = pl.BlockSpec(memory_space=pl.ANY)
-    sem = pltpu.SemaphoreType.DMA
-    p_all, s_all, cols = pl.pallas_call(
-        front,
-        out_shape=(
-            jax.ShapeDtypeStruct((NX, 2, RB, KP, T, T), BF16),
-            jax.ShapeDtypeStruct((8, 4, ROWS, T), BF16),
-            jax.ShapeDtypeStruct((NX, 2, 1, T), jnp.int32),
-        ),
-        in_specs=[vmem, vmem],
-        out_specs=(anys, anys, anys),
+    vmem, sem = pltpu.VMEM, pltpu.SemaphoreType.DMA
+    return pl.pallas_call(
+        step,
+        out_shape=jax.ShapeDtypeStruct((Q, 64 * T), F32),
+        in_specs=[pl.BlockSpec(memory_space=pl.ANY), pl.BlockSpec(memory_space=pltpu.VMEM)],
+        out_specs=pl.BlockSpec(memory_space=pltpu.VMEM),
         scratch_shapes=[
-            pltpu.VMEM((NX, 2, RB, KP, T, T), BF16),
-            pltpu.VMEM((NZ, KP + 1, Q, T), BF16),
-            pltpu.VMEM((NZ, 1, T), jnp.int32),
-            pltpu.VMEM((NX, 2, 1, T), jnp.int32),
-            pltpu.VMEM((NZ, 1, T), jnp.int32),
+            vmem((RB, KP, T, T), BF16),
+            vmem((RB, 1, T), jnp.int32),
+            vmem((NX, 2, RB, KP, T, T), BF16),
+            vmem((NZ, KP + 1, Q, T), BF16),
+            vmem((NZ, 1, T), jnp.int32),
+            vmem((NX, 2, RB, 1, T), jnp.int32),
+            vmem((NZ, 1, T), jnp.int32),
             pltpu.SMEM((NZ, 1, T), jnp.int32),
-            pltpu.SMEM((NX, 2, 1, T), jnp.int32),
-            pltpu.VMEM((8, 4, ROWS, T), F32),
-            pltpu.VMEM((8, 4, ROWS, T), BF16),
-            pltpu.VMEM((8, 2, HALF, T), BF16),
-            pltpu.VMEM((8, 4, HALF, T), BF16),
-            pltpu.VMEM((8, 2, HALF, T), BF16),
-            pltpu.VMEM((8, 4, ROWS, T), BF16),
+            pltpu.SMEM((NX, 2, RB, 1, T), jnp.int32),
+            vmem((8, 4, ROWS, T), F32),
+            vmem((8, 4, ROWS, T), BF16),
+            vmem((8, 2, HALF, T), BF16),
+            vmem((8, 4, HALF, T), BF16),
+            vmem((8, 2, HALF, T), BF16),
+            vmem((8, 4, ROWS, T), BF16),
+            vmem((2 * NX * RB, T), jnp.int32),
+            vmem((2 * NX * RB, T), jnp.int32),
+            vmem((3, 1, T), jnp.int32),
+            pltpu.SMEM((3, 1, T), jnp.int32),
+            vmem((TILES, ROWS, T), F32),
+            vmem((2, TILES + 9, Q, T), F32),
+            vmem((2, 4, SUBS, PER, Q, T), BF16),
+            vmem((2, 4, SUBS, PER, Q, T), BF16),
             sem((3, 2)), sem((3, 2)), sem((4, 2)), sem((4, 2)),
             sem((7,)), sem((7,)), sem((8,)), sem((2,)),
             sem((2, NZ)), sem((2, NZ)), sem((8, 12)), sem((8, 12)),
-            sem((2,)), sem((13,)),
+            sem((3,)), sem((2, 4, SUBS)), sem((2, 4, SUBS)),
         ],
         compiler_params=pltpu.CompilerParams(
-            collective_id=0, has_side_effects=True, vmem_limit_bytes=40 << 20),
-        name="front",
-    )(v, cflat)
-    r_all = pl.pallas_call(
-        middle,
-        out_shape=jax.ShapeDtypeStruct((NZ, 64, Q, T), BF16),
-        grid=(8,),
-        in_specs=[
-            pl.BlockSpec(memory_space=pltpu.SMEM),
-            pl.BlockSpec((1, 1, RB, KP, T, T), lambda n: (n // 2, n % 2, 0, 0, 0, 0)),
-            pl.BlockSpec((2, 4, ROWS, T), lambda n: (n // 2, 0, 0, 0)),
-        ],
-        out_specs=vmem,
-        scratch_shapes=[pltpu.VMEM((64, ROWS, T), F32)],
-        compiler_params=pltpu.CompilerParams(
-            dimension_semantics=("arbitrary",), vmem_limit_bytes=40 << 20),
-        name="middle",
-    )(cols, p_all, s_all)
-    return pl.pallas_call(
-        back,
-        out_shape=jax.ShapeDtypeStruct((Q, 64 * T), F32),
-        in_specs=[vmem],
-        out_specs=vmem,
-        scratch_shapes=[
-            pltpu.VMEM((2, 4, SUBS, PER, Q, T), BF16),
-            pltpu.VMEM((2, 4, SUBS, PER, Q, T), BF16),
-            sem((2, 4, SUBS)), sem((2, 4, SUBS)),
-        ],
-        compiler_params=pltpu.CompilerParams(
-            collective_id=1, has_side_effects=True, vmem_limit_bytes=40 << 20),
-        name="back",
-    )(r_all)
+            collective_id=0, has_side_effects=True, vmem_limit_bytes=61 << 20),
+        name="step",
+    )(block_values.reshape(RB, KP, T, T), block_cols)
 
 
 def solution(mesh):

time: 134 us -> 125 us (0.933); the launches traced: 134 us -> 123 us
  Pallas kernels: 130 us -> 121 us
  other arithmetic: 1.34 us -> 0 us
    pallas_call x3 -> x1, Pallas kernels: 130 us -> 121 us  [local(): pl.pallas_call(step, out_shape=jax.ShapeDtypeStruct((Q, 64 * T), F32), in...]
    unnamed x1 -> x0, other arithmetic: 1.34 us -> none
where the time goes in v2:
time: 125 us; the launch traced here: 123 us
  Pallas kernels  121 us (97%)
  local copies, waits for them, and re-layouts  2.26 us (2%)
    pallas_call x1, Pallas kernels, local(): pl.pallas_call(step, out_shape=jax.ShapeDtypeStruct((Q, 64 * T), F32), in...  121 us

profile of v2, /device:TPU:1, one launch (start us, length us, event | category | flops | bytes accessed | tf_op | source)
XLA Modules:
  0.0 122.9 jit_solution(9333765027019610262)
XLA Ops:
  0.0 120.6 %step.1 = f32[32,8192]{1,0:T(8,128)} custom-call(bf16[4,6,128,128]{3,2,1,0:T(8,128)(2,1)} %bitcast.1, s32[1,4,1,6]{3,2,1,0:T(1,128)} %c_in.1), custom_call_target="tpu_custom_call" | custom-call | tf_op jit(solution)/shard_map/step/pallas_call | solution.py:501
  120.6 2.3 %copy.4 = f32[32,8192]{1,0:T(8,128)} copy(f32[32,8192]{1,0:T(8,128)} %step.1) | data formatting | bytes 2097152

commit v3 on v2

v3 whole, which is shorter than its diff:
```python
import functools

import jax
import jax.numpy as jnp
from jax import lax
from jax.experimental import pallas as pl
from jax.experimental.pallas import tpu as pltpu
from jax.sharding import PartitionSpec as P

MESH = pl.DeviceIdType.MESH
F32, BF16 = jnp.float32, jnp.bfloat16
NZ, NX, NY = 8, 4, 4
RB, KP, T = 4, 6, 128
Q = T // NX
ROWS = NZ * Q
HALF = ROWS // 2
OFFSETS = (4, 3, -3, 2, -2, 1, -1, 0)
OWN = 7
THREE = 3 * Q
VMEM_MIB = 51
TILES = NX * 2 * RB * KP
SUBS = 8
PER = 64 // SUBS


def where_am_i():
    g = lax.axis_index("gx")
    return g // 2, lax.rem(g, 2), lax.axis_index("gy"), lax.axis_index("gz")


def at_z(z, c):
    return {"gx": lax.rem(z + 2 * NZ, NZ) * 2 + c}


def greet(devices):
    barrier = pltpu.get_barrier_semaphore()
    for device in devices:
        pl.semaphore_signal(barrier, inc=1, device_id=device, device_id_type=MESH)
    pl.semaphore_wait(barrier, len(devices))


def nt_dot(a, b):
    return lax.dot_general(a, b, (((1,), (1,)), ((), ())), preferred_element_type=F32)


def sort_tiles(cp, colv, prev, ordv):
    for n in range(2 * NX * RB):
        colv[n : n + 1, :] = cp[n // 8, n // 4 % 2, n % 4]
    count = 2 * NX * RB
    cols = colv[...]
    lanes = lax.broadcasted_iota(jnp.int32, (count, T), 1)
    hits = [jnp.broadcast_to(cols[:, k : k + 1], (count, T)) == lanes for k in range(KP)]
    listed = jnp.zeros((count, T), jnp.int32)
    for hit in hits:
        listed = listed + jnp.where(hit, 1, 0)
    run = jnp.zeros((1, T), jnp.int32)
    for n in range(count):
        prev[n : n + 1, :] = run
        run = run + listed[n : n + 1, :]
    lane = lax.broadcasted_iota(jnp.int32, (1, T), 1)
    upto = run
    for shift in (1, 2, 4, 8, 16, 32, 64):
        upto = upto + jnp.where(lane >= shift, pltpu.roll(upto, shift, 1), 0)
    before = prev[...]
    place = (jnp.broadcast_to(upto - run, (count, T)) + before) * 2 + jnp.where(before > 0, 1, 0)
    ordv[2] = jnp.where(run > 0, upto - 1, TILES)
    tile = lax.broadcasted_iota(jnp.int32, (count, T), 0) * KP
    picked = [jnp.zeros((count, T), jnp.int32) for part in range(2)]
    for k, hit in enumerate(hits):
        mine = jnp.sum(jnp.where(hit, place, 0), axis=1, keepdims=True)
        mine = jnp.broadcast_to(mine, (count, T))
        code = (tile + k) * 2 + jnp.where(lax.rem(mine, 2) == 1, 1, 0)
        for part in range(2):
            picked[part] = jnp.where(mine // 2 == lanes + part * T, code, picked[part])
    for part in range(2):
        ordv[part] = jnp.sum(picked[part], axis=0, keepdims=True)


def step(v_hbm, c_in, o_ref,
         c_ref, pall, lfar, lnear, cw, cp, mapv, maps, cps, sb, relay, parts, dparts, fwd, sfin,
         colv, prev, ordv, ords, prods, sums, rbuf, sbuf,
         xs, xr, ds, dr, cs, cr, ls, lr, ws, wr, ys, yr, loc, zs, zr):
    z, c, x, y = where_am_i()
    xright, xleft = lax.rem(x + 1, NX), lax.rem(x + 3, NX)
    yright, yleft, yopp = lax.rem(y + 1, NY), lax.rem(y + 3, NY), lax.rem(y + 2, NY)
    sib = {"gx": z * 2 + 1 - c}

    def remote(src, dst, ssem, rsem, device):
        return pltpu.make_async_remote_copy(
            src_ref=src, dst_ref=dst, send_sem=ssem, recv_sem=rsem,
            device_id=device, device_id_type=MESH)

    v_ref = pall.at[0, c]
    fetch = pltpu.make_async_copy(v_hbm, v_ref, loc.at[2])
    fetch.start()
    for r in range(RB):
        c_ref[r] = jnp.zeros((1, T), jnp.int32)
        c_ref[r, :, 0:KP] = c_in[0, r]

    col_peers = []
    for dx in range(NX):
        for dc in range(2):
            if dx or dc:
                col_peers.append((dx, dc, {"gx": z * 2 + lax.rem(c + dc, 2), "gy": lax.rem(x + dx, NX)}))
    greet([p[2] for p in col_peers] + [at_z(z + d, c) for d in range(1, NZ)]
          + [{"gz": yright}, {"gz": yleft}, {"gz": yopp}])
    fetch.wait()
    started = []

    def slot(p):
        return lfar.at[p] if p < 5 else lnear.at[p - 5]

    def go(copy):
        copy.start()
        started.append(copy)
        return copy

    csend = []
    for n, (dx, dc, dev) in enumerate(col_peers):
        rel = {0: 0, 1: 1, 2: 3, 3: 2}[dx]
        csend.append(go(remote(c_ref, cp.at[rel, c], cs.at[n], cr.at[n], dev)))
    cp[0, c] = c_ref[...]

    def left_copy(dx):
        return remote(v_ref.at[0, :, pl.ds(dx * Q, Q), :], lnear.at[OWN - 5, 0:KP], ls.at[dx], lr.at[0], {"gy": dx})

    def leftc_copy(dx):
        return remote(c_ref.at[0], cw.at[OWN], ls.at[NX + dx], lr.at[1], {"gy": dx})

    @pl.when(x == 0)
    def _():
        for dx in (2, 1, 3):
            leftc_copy(dx).start()
        for dx in (2, 1, 3):
            left_copy(dx).start()

    xsend, dsend = {}, {}
    for order in range(2):
        for way, half, dev in ((0, order, xright), (1, 1 - order, xleft)):
            rows = pl.ds(2 * half, 2)
            xsend[way, half] = go(remote(v_ref.at[rows], pall.at[1 + way, c, rows],
                                         xs.at[way, half], xr.at[way, half], {"gy": dev}))
    for half in range(2):
        rows = pl.ds(2 * half, 2)
        dsend[0, half] = go(remote(v_ref.at[rows], v_ref.at[rows], ds.at[0, half], dr.at[0, half], sib))
    for p in range(NZ):
        slot(p)[KP] = jnp.zeros((Q, T), BF16)

    @pl.when(x == 0)
    def _():
        lnear[OWN - 5, 0:KP] = pall[0, c, 0, :, 0:Q, :]
        cw[OWN] = c_ref[0]

    @pl.when(x != 0)
    def _():
        leftc_copy(0).wait_recv()

    ring = [(off, OFFSETS.index(off), at_z(z - off, c)) for off in (1, -1, -2, 2, 3, -3, 4)]
    wcsend = {p: go(remote(cw.at[OWN], cw.at[p], ws.at[1, p], wr.at[1, p], dev)) for off, p, dev in ring}

    @pl.when(x != 0)
    def _():
        left_copy(0).wait_recv()

    wsend = {p: go(remote(slot(OWN).at[0:KP], slot(p).at[0:KP], ws.at[0, p], wr.at[0, p], dev)) for off, p, dev in ring}
    for copy in csend:
        copy.wait_recv()
    cols_copy = pltpu.make_async_copy(cp, cps, loc.at[0])
    cols_copy.start()
    lane = lax.broadcasted_iota(jnp.int32, (1, T), 1)

    def windows(first, last):
        for p in range(first, last):
            if p != OWN:
                wcsend[p].wait_recv()
            row = cw[p]
            found = jnp.full((1, T), KP, jnp.int32)
            for k in range(KP):
                found = jnp.where(jnp.broadcast_to(row[:, k : k + 1], (1, T)) == lane, k, found)
            mapv[p] = found
        some = pl.ds(first, last - first)
        copy = pltpu.make_async_copy(mapv.at[some], maps.at[some], loc.at[1])
        copy.start()
        for p in range(first, last):
            if p != OWN:
                wsend[p].wait_recv()
        copy.wait()

    direct = []
    R, L, OPP = {"gz": yright}, {"gz": yleft}, {"gz": yopp}

    def squares(jobs):
        def body(n, carry):
            block, r = n // 2, lax.rem(n, 2)
            for u, r0, size in jobs:
                rel, row = u // 2, 2 * (u % 2) + r
                wide = []
                for k in range(KP):
                    col = cps[rel, block, row, 0, k]
                    wide.append(jnp.concatenate(
                        [slot(p)[maps[p, 0, col]] for p in range(r0 // Q, (r0 + size) // Q)], axis=0))
                total = None
                for k in range(0, KP, 2):
                    lhs = jnp.concatenate(wide[k : k + 2], axis=1)
                    rhs = jnp.concatenate([pall[rel, block, row, k], pall[rel, block, row, k + 1]], axis=1)
                    prod = nt_dot(lhs, rhs)
                    total = prod if total is None else total + prod
                sb[u, n, r0 : r0 + size] = total.astype(BF16)
            return carry

        lax.fori_loop(0, 4, body, 0)
        for job in jobs:
            for m in range(3) if job in direct else range(4):
                go(message(job, m))


    def message(job, m):
        u, r0, size = job
        n, h = u * 2 + (1 if r0 else 0), size // 2
        top, bottom = pl.ds(r0, h), pl.ds(r0 + h, h)
        part = pl.ds(r0 // 2, h)
        if job in direct:
            dev = (R, L, OPP)[m % 3]
            if m < 3:
                src, dst = sb.at[u, (yright, yleft, yopp)[m], pl.ds(r0, size)], dparts.at[u % 2, m]
            else:
                src = dst = sfin.at[u, y, pl.ds(r0, size)]
        elif m == 0:
            src, dst, dev = sb.at[u, yopp, bottom], relay.at[u, 0, part], R
        elif m == 1:
            src, dst, dev = sb.at[u, yopp, top], relay.at[u, 1, part], L
        elif m == 2:
            src, dst, dev = sb.at[u, yright, top], parts.at[u, 0, part], R
        elif m == 3:
            src, dst, dev = sb.at[u, yleft, bottom], parts.at[u, 1, part], L
        elif m == 4:
            src, dst, dev = fwd.at[u, 0, part], parts.at[u, 2, part], R
        elif m == 5:
            src, dst, dev = fwd.at[u, 1, part], parts.at[u, 3, part], L
        elif m < 10:
            src = dst = sfin.at[u, y, top if m in (6, 8) else bottom]
            dev = R if m < 8 else L
        elif m == 10:
            src = dst = sfin.at[u, yleft, top]
            dev = R
        else:
            src = dst = sfin.at[u, yright, bottom]
            dev = L
        return remote(src, dst, ys.at[n, m], yr.at[n, m], dev)

    def send_relay(job):
        u, r0, size = job
        q, h = r0 // 2, size // 2
        message(job, 0).wait_recv()
        fwd[u, 0, q : q + h] = (sb[u, yright, r0 + h : r0 + size].astype(F32) + relay[u, 0, q : q + h].astype(F32)).astype(BF16)
        go(message(job, 4))
        message(job, 1).wait_recv()
        fwd[u, 1, q : q + h] = (sb[u, yleft, r0 : r0 + h].astype(F32) + relay[u, 1, q : q + h].astype(F32)).astype(BF16)
        go(message(job, 5))

    def send_sum(job):
        u, r0, size = job
        q, h = r0 // 2, size // 2
        message(job, 2).wait_recv()
        message(job, 5).wait_recv()
        sfin[u, y, r0 : r0 + h] = (
            sb[u, y, r0 : r0 + h].astype(F32) + parts[u, 0, q : q + h].astype(F32) + parts[u, 3, q : q + h].astype(F32)).astype(BF16)
        go(message(job, 6))
        go(message(job, 8))
        message(job, 3).wait_recv()
        message(job, 4).wait_recv()
        sfin[u, y, r0 + h : r0 + size] = (
            sb[u, y, r0 + h : r0 + size].astype(F32) + parts[u, 1, q : q + h].astype(F32) + parts[u, 2, q : q + h].astype(F32)).astype(BF16)
        go(message(job, 9))
        go(message(job, 7))

    def send_sum_direct(job):
        u, r0, size = job
        total = sb[u, y, r0 : r0 + size].astype(F32)
        for m in range(3):
            message(job, m).wait_recv()
            total = total + dparts[u % 2, m].astype(F32)
        sfin[u, y, r0 : r0 + size] = total.astype(BF16)
        for m in range(3, 6):
            go(message(job, m))

    def send_forward(job):
        message(job, 6).wait_recv()
        go(message(job, 10))
        message(job, 9).wait_recv()
        go(message(job, 11))

    def products(jobs):
        for job in jobs:
            for m in (3, 4, 5) if job in direct else (7, 8, 10, 11):
                message(job, m).wait_recv()

        def body(n, carry):
            block, r = n // 2, lax.rem(n, 2)
            for u, r0, size in jobs:
                rel, row = u // 2, 2 * (u % 2) + r
                wide = jnp.concatenate([pall[rel, block, row, k] for k in range(KP)], axis=1)
                both = jnp.dot(sfin[u, n, r0 : r0 + size], wide, preferred_element_type=F32)
                at = ((rel * 2 + block) * RB + row) * KP
                for k in range(KP):
                    prods[at + k, r0 : r0 + size] = both[:, k * T : (k + 1) * T]
            return carry

        lax.fori_loop(0, 4, body, 0)

    def arrive(rel, half):
        rows = pl.ds(2 * half, 2)
        dsend[rel, half] = go(remote(pall.at[rel, c, rows], pall.at[rel, c, rows],
                                     ds.at[rel, half], dr.at[rel, half], sib))

    def each(what, jobs):
        for job in jobs:
            what(job)

    def both_cores(units):
        for key in units:
            dsend[key].wait_recv()

    def jobs_of(units, r0, size):
        return [(rel * 2 + half, r0, size) for rel, half in units]

    O, A, B, C = ((0, 0), (0, 1)), ((1, 0), (2, 1)), ((1, 1), (2, 0)), ((3, 0), (3, 1))
    ofar, onear = jobs_of(O, 0, ROWS - THREE), jobs_of(O, ROWS - THREE, THREE)
    afar, anear = jobs_of(A, 0, ROWS - THREE), jobs_of(A, ROWS - THREE, THREE)
    bfar, brest = jobs_of(B, 0, THREE), jobs_of(B, THREE, ROWS - THREE)
    cfar, crest = jobs_of(C, 0, THREE), jobs_of(C, THREE, ROWS - THREE)
    direct.extend(cfar)
    cols_copy.wait()
    windows(5, 8)
    both_cores(O)
    squares(onear)
    rows = pl.ds(0, 2)
    xsend[0, 0].wait_recv()
    xsend[2, 0] = go(remote(pall.at[1, c, rows], pall.at[3, c, rows], xs.at[2, 0], xr.at[2, 0], {"gy": xright}))
    arrive(1, 0)
    rows = pl.ds(2, 2)
    xsend[1, 1].wait_recv()
    xsend[2, 1] = go(remote(pall.at[2, c, rows], pall.at[3, c, rows], xs.at[2, 1], xr.at[2, 1], {"gy": xleft}))
    arrive(2, 1)
    each(send_relay, onear)
    both_cores(A)
    squares(anear)
    windows(0, 5)
    squares(ofar)
    each(send_sum, onear)
    squares(afar)
    each(send_relay, anear)
    each(send_relay, ofar)
    xsend[0, 1].wait_recv()
    arrive(1, 1)
    xsend[1, 0].wait_recv()
    arrive(2, 0)
    each(send_forward, onear)
    each(send_sum, anear)
    both_cores(B)
    squares(bfar)
    each(send_relay, afar)
    each(send_sum, ofar)
    squares(brest)
    each(send_forward, anear)
    each(send_relay, bfar)
    each(send_sum, afar)
    each(send_forward, ofar)
    xsend[2, 0].wait_recv()
    arrive(3, 0)
    xsend[2, 1].wait_recv()
    arrive(3, 1)
    each(send_sum, bfar)
    both_cores(C)
    squares(cfar)
    squares(crest)
    each(send_forward, afar)
    each(send_relay, brest)
    each(send_forward, bfar)
    sort_tiles(cp, colv, prev, ordv)
    order_copy = pltpu.make_async_copy(ordv, ords, loc.at[0])
    order_copy.start()
    products(ofar)
    each(send_sum_direct, cfar)
    each(send_sum, brest)
    products(afar)
    each(send_relay, crest)
    order_copy.wait()
    products(bfar)

    zdevs = (at_z(z + 1, c), at_z(z - 1, c))
    ahead = lax.rem(y - x + NX, NX)
    here = jnp.where(ahead == 0, 0, jnp.where(ahead == 3, 1, jnp.where(ahead == 1, 2, 3)))

    def scan(way, p):
        rows = slice(p * Q, p * Q + Q)
        run = jnp.zeros((Q, T), F32)
        for part in range(2):
            def body(n, run, part=part):
                for m in range(8):
                    t = n * 8 + m
                    code = ords[part, 0, t]
                    tile = prods[code // 2, rows]
                    run = tile + run * lax.rem(code, 2).astype(F32)
                    sums[way, part * T + t] = run
                return run

            run = lax.fori_loop(0, 16 if part == 0 else TILES // 8 - 16, body, run)
        for n in range(2 * RB):
            last = ords[2, 0, 8 * z + n]
            mine = sfin[here * 2 + n % 4 // 2, n // 4 * 2 + n % 2, rows].astype(F32)
            sums[way, TILES + 1 + n] = sums[way, last] - 1.5 * mine

    def result_tile(way, j):
        own = j - 8 * z
        inside = jnp.logical_and(own >= 0, own < 8)
        return -2.0 * sums[way, jnp.where(inside, TILES + 1 + own, ords[2, 0, j])]

    def zcopy(way, hop, sub):
        return remote(sbuf.at[way, hop % 2, sub], rbuf.at[way, hop, sub],
                      zs.at[way, hop, sub], zr.at[way, hop, sub], zdevs[way])

    def emit(way, hop, sub, have, again=False):
        if again:
            zcopy(way, hop - 2, sub).wait_send()
        if have:
            zcopy(way, hop - 1, sub).wait_recv()
        for t in range(PER):
            tile = result_tile(0 if hop == 0 else way, sub * PER + t)
            if have:
                tile = tile + rbuf[way, hop - 1, sub, t].astype(F32)
            sbuf[way, hop % 2, sub, t] = tile.astype(BF16)
        zcopy(way, hop, sub).start()

    for way in range(2):
        sums[way, TILES] = jnp.zeros((Q, T), F32)
    hs = SUBS // 2
    products(cfar)
    scan(0, 0)

    def hop0(n, carry):
        emit(0, 0, n, False)
        emit(1, 0, n + hs, False)
        return carry

    lax.fori_loop(0, hs, hop0, 0)
    for hop in range(1, 4):
        if hop == 1:
            each(send_forward, brest)
            each(send_sum, crest)
        if hop == 2:
            products(anear)
            products(brest)
            products(crest)
        scan(0, 2 * hop - 1)
        scan(1, 2 * hop)
        if hop == 1:
            products(onear)
            each(send_forward, crest)

        def fresh(n, carry, hop=hop):
            emit(0, hop, n + hs, hop > 1, hop == 3)
            emit(1, hop, n, hop > 1, hop == 3)
            return carry

        def relayed(n, carry, hop=hop):
            emit(0, hop, n, True, hop > 1)
            emit(1, hop, n + hs, True, hop > 1)
            return carry

        lax.fori_loop(0, hs, fresh, 0)
        lax.fori_loop(0, hs, relayed, 0)
    scan(0, OWN)
    for n in range(SUBS):
        sub = n // 2 + hs * (n % 2)
        for way in range(2):
            zcopy(way, 3, sub).wait_recv()
        for t in range(PER):
            j = sub * PER + t
            tile = result_tile(0, j) + rbuf[0, 3, sub, t].astype(F32) + rbuf[1, 3, sub, t].astype(F32)
            o_ref[:, j * T : (j + 1) * T] = tile

    @pl.when(x == 0)
    def _():
        for dx in range(1, NX):
            left_copy(dx).wait_send()
            leftc_copy(dx).wait_send()

    def drain(n, carry):
        for way in range(2):
            for hop in range(2, 4):
                zcopy(way, hop, n).wait_send()
        return carry

    lax.fori_loop(0, SUBS, drain, 0)

    for copy in started:
        copy.wait_send()


def local(block_values, block_cols):
    vmem, sem = pltpu.VMEM, pltpu.SemaphoreType.DMA
    return pl.pallas_call(
        step,
        out_shape=jax.ShapeDtypeStruct((Q, 64 * T), F32),
        in_specs=[pl.BlockSpec(memory_space=pltpu.HBM), pl.BlockSpec(memory_space=pltpu.VMEM)],
        out_specs=pl.BlockSpec(memory_space=pltpu.VMEM),
        scratch_shapes=[
            vmem((RB, 1, T), jnp.int32),
            vmem((NX, 2, RB, KP, T, T), BF16),
            vmem((5, KP + 1, Q, T), BF16),
            vmem((3, KP + 1, Q, T), BF16),
            vmem((NZ, 1, T), jnp.int32),
            vmem((NX, 2, RB, 1, T), jnp.int32),
            vmem((NZ, 1, T), jnp.int32),
            pltpu.SMEM((NZ, 1, T), jnp.int32),
            pltpu.SMEM((NX, 2, RB, 1, T), jnp.int32),
            vmem((8, 4, ROWS, T), BF16),
            vmem((8, 2, HALF, T), BF16),
            vmem((8, 4, HALF, T), BF16),
            vmem((2, 3, THREE, T), BF16),
            vmem((8, 2, HALF, T), BF16),
            vmem((8, 4, ROWS, T), BF16),
            vmem((2 * NX * RB, T), jnp.int32),
            vmem((2 * NX * RB, T), jnp.int32),
            vmem((3, 1, T), jnp.int32),
            pltpu.SMEM((3, 1, T), jnp.int32),
            vmem((TILES, ROWS, T), F32),
            vmem((2, TILES + 9, Q, T), F32),
            vmem((2, 4, SUBS, PER, Q, T), BF16),
            vmem((2, 2, SUBS, PER, Q, T), BF16),
            sem((3, 2)), sem((3, 2)), sem((4, 2)), sem((4, 2)),
            sem((7,)), sem((7,)), sem((8,)), sem((2,)),
            sem((2, NZ)), sem((2, NZ)), sem((16, 12)), sem((16, 12)),
            sem((3,)), sem((2, 4, SUBS)), sem((2, 4, SUBS)),
        ],
        compiler_params=pltpu.CompilerParams(
            collective_id=0, has_side_effects=True, vmem_limit_bytes=VMEM_MIB << 20),
        name="step",
    )(block_values.reshape(RB, KP, T, T), block_cols)


def solution(mesh):
    in_specs = (P("gy", "gx", "gz", None, None, None), P("gy", "gx", "gz", None))
    return jax.shard_map(local, mesh=mesh, in_specs=in_specs, out_specs=P(("gx", "gy"), "gz"), check_vma=False)
```

time: 125 us -> 109 us (0.87); the launches traced: 123 us -> 109 us
  Pallas kernels: 121 us -> 106 us
    pallas_call x1, Pallas kernels: 121 us -> 106 us  [local(): pl.pallas_call(step, out_shape=jax.ShapeDtypeStruct((Q, 64 * T), F32), in...]
    unnamed x1 -> x5, local copies, waits for them, and re-layouts: 2.26 us -> 2.79 us
where the time goes in v3:
time: 109 us
  Pallas kernels  106 us (97%)
  local copies, waits for them, and re-layouts  2.79 us (3%)
    pallas_call x1, Pallas kernels, local(): pl.pallas_call(step, out_shape=jax.ShapeDtypeStruct((Q, 64 * T), F32), in...  106 us
    unnamed x5, local copies, waits for them, and re-layouts  2.79 us

profile of v3, /device:TPU:1, one launch (start us, length us, event | category | flops | bytes accessed | tf_op | source)
XLA Modules:
  0.0 108.9 jit_solution(12816661902936624431)
XLA Ops:
  0.0 0.0 copy-start
  0.0 1.1 %copy-done = bf16[1,4,1,6,128,128]{5,4,3,2,1,0:T(8,128)(2,1)S(1)} copy-done((bf16[1,4,1,6,128,128]{5,4,3,2,1,0:T(8,128)(2,1)S(1)}, bf16[1,4,1,6,128,128]{5,4,3,2,1,0:T(8,128)(2,1)}, u32[]{:S(2)}) %copy-start) | copy-done | bytes 786456
  1.1 0.0 copy-start.1
  1.1 0.7 copy-done.1
  1.8 106.1 %step.1 = f32[32,8192]{1,0:T(8,128)S(1)} custom-call(bf16[4,6,128,128]{3,2,1,0:T(8,128)(2,1)S(1)} %bitcast.1, s32[1,4,1,6]{3,2,1,0:T(1,128)S(1)} %copy-done.1), custom_call_target="tpu_custom_call" | custom-call | tf_op jit(solution)/shard_map/step/pallas_call | solution.py:503
  107.9 1.0 copy.4
Async XLA Ops:
  0.0 1.1 %copy-start = (bf16[1,4,1,6,128,128]{5,4,3,2,1,0:T(8,128)(2,1)S(1)}, bf16[1,4,1,6,128,128]{5,4,3,2,1,0:T(8,128)(2,1)}, u32[]{:S(2)}) copy-start(bf16[1,4,1,6,128,128]{5,4,3,2,1,0:T(8,128)(2,1)} %param.2) | copy-start | bytes 2359300
  1.1 0.7 copy-start.1

commit v4 on v3

--- a/solution.py
+++ b/solution.py
@@ -169,7 +169,7 @@
     cols_copy.start()
     lane = lax.broadcasted_iota(jnp.int32, (1, T), 1)
 
-    def windows(first, last):
+    def slots_of(first, last, sem):
         for p in range(first, last):
             if p != OWN:
                 wcsend[p].wait_recv()
@@ -179,17 +179,27 @@
                 found = jnp.where(jnp.broadcast_to(row[:, k : k + 1], (1, T)) == lane, k, found)
             mapv[p] = found
         some = pl.ds(first, last - first)
-        copy = pltpu.make_async_copy(mapv.at[some], maps.at[some], loc.at[1])
+        copy = pltpu.make_async_copy(mapv.at[some], maps.at[some], sem)
         copy.start()
+        return copy
+
+    def windows(first, last):
         for p in range(first, last):
             if p != OWN:
                 wsend[p].wait_recv()
-        copy.wait()
 
     direct = []
     R, L, OPP = {"gz": yright}, {"gz": yleft}, {"gz": yopp}
 
-    def squares(jobs):
+    def each(what, jobs):
+        for job in jobs:
+            what(job)
+
+    def send_parts(job):
+        for m in range(3) if job in direct else range(4):
+            go(message(job, m))
+
+    def squares(jobs, send=True):
         def body(n, carry):
             block, r = n // 2, lax.rem(n, 2)
             for u, r0, size in jobs:
@@ -209,9 +219,8 @@
             return carry
 
         lax.fori_loop(0, 4, body, 0)
-        for job in jobs:
-            for m in range(3) if job in direct else range(4):
-                go(message(job, m))
+        if send:
+            each(send_parts, jobs)
 
 
     def message(job, m):
@@ -222,7 +231,7 @@
         if job in direct:
             dev = (R, L, OPP)[m % 3]
             if m < 3:
-                src, dst = sb.at[u, (yright, yleft, yopp)[m], pl.ds(r0, size)], dparts.at[u % 2, m]
+                src, dst = sb.at[u, (yright, yleft, yopp)[m], pl.ds(r0, size)], dparts.at[direct.index(job), m]
             else:
                 src = dst = sfin.at[u, y, pl.ds(r0, size)]
         elif m == 0:
@@ -279,7 +288,7 @@
         total = sb[u, y, r0 : r0 + size].astype(F32)
         for m in range(3):
             message(job, m).wait_recv()
-            total = total + dparts[u % 2, m].astype(F32)
+            total = total + dparts[direct.index(job), m].astype(F32)
         sfin[u, y, r0 : r0 + size] = total.astype(BF16)
         for m in range(3, 6):
             go(message(job, m))
@@ -313,10 +322,6 @@
         dsend[rel, half] = go(remote(pall.at[rel, c, rows], pall.at[rel, c, rows],
                                      ds.at[rel, half], dr.at[rel, half], sib))
 
-    def each(what, jobs):
-        for job in jobs:
-            what(job)
-
     def both_cores(units):
         for key in units:
             dsend[key].wait_recv()
@@ -329,11 +334,17 @@
     afar, anear = jobs_of(A, 0, ROWS - THREE), jobs_of(A, ROWS - THREE, THREE)
     bfar, brest = jobs_of(B, 0, THREE), jobs_of(B, THREE, ROWS - THREE)
     cfar, crest = jobs_of(C, 0, THREE), jobs_of(C, THREE, ROWS - THREE)
-    direct.extend(cfar)
+    direct.extend(bfar + cfar)
     cols_copy.wait()
+    near_slots = slots_of(5, 8, loc.at[1])
     windows(5, 8)
+    near_slots.wait()
     both_cores(O)
     squares(onear)
+    far_slots = slots_of(0, 5, loc.at[3])
+    sort_tiles(cp, colv, prev, ordv)
+    order_copy = pltpu.make_async_copy(ordv, ords, loc.at[0])
+    order_copy.start()
     rows = pl.ds(0, 2)
     xsend[0, 0].wait_recv()
     xsend[2, 0] = go(remote(pall.at[1, c, rows], pall.at[3, c, rows], xs.at[2, 0], xr.at[2, 0], {"gy": xright}))
@@ -343,6 +354,7 @@
     xsend[2, 1] = go(remote(pall.at[2, c, rows], pall.at[3, c, rows], xs.at[2, 1], xr.at[2, 1], {"gy": xleft}))
     arrive(2, 1)
     each(send_relay, onear)
+    far_slots.wait()
     both_cores(A)
     squares(anear)
     windows(0, 5)
@@ -355,38 +367,28 @@
     arrive(1, 1)
     xsend[1, 0].wait_recv()
     arrive(2, 0)
-    each(send_forward, onear)
-    each(send_sum, anear)
+    each(send_relay, afar)
     both_cores(B)
     squares(bfar)
-    each(send_relay, afar)
     each(send_sum, ofar)
-    squares(brest)
-    each(send_forward, anear)
-    each(send_relay, bfar)
     each(send_sum, afar)
-    each(send_forward, ofar)
     xsend[2, 0].wait_recv()
     arrive(3, 0)
     xsend[2, 1].wait_recv()
     arrive(3, 1)
-    each(send_sum, bfar)
+    each(send_sum_direct, bfar)
     both_cores(C)
     squares(cfar)
+    each(send_forward, ofar)
+    each(send_forward, afar)
+    squares(brest, send=False)
+    each(send_sum_direct, cfar)
+    each(send_parts, brest)
+    products(ofar)
+    products(bfar)
     squares(crest)
-    each(send_forward, afar)
-    each(send_relay, brest)
-    each(send_forward, bfar)
-    sort_tiles(cp, colv, prev, ordv)
-    order_copy = pltpu.make_async_copy(ordv, ords, loc.at[0])
-    order_copy.start()
-    products(ofar)
-    each(send_sum_direct, cfar)
-    each(send_sum, brest)
     products(afar)
-    each(send_relay, crest)
     order_copy.wait()
-    products(bfar)
 
     zdevs = (at_z(z + 1, c), at_z(z - 1, c))
     ahead = lax.rem(y - x + NX, NX)
@@ -446,17 +448,15 @@
     lax.fori_loop(0, hs, hop0, 0)
     for hop in range(1, 4):
         if hop == 1:
-            each(send_forward, brest)
-            each(send_sum, crest)
+            each(send_forward, onear)
+            each(send_sum, anear)
+            each(send_relay, brest)
+            each(send_relay, crest)
         if hop == 2:
-            products(anear)
             products(brest)
             products(crest)
         scan(0, 2 * hop - 1)
         scan(1, 2 * hop)
-        if hop == 1:
-            products(onear)
-            each(send_forward, crest)
 
         def fresh(n, carry, hop=hop):
             emit(0, hop, n + hs, hop > 1, hop == 3)
@@ -469,7 +469,18 @@
             return carry
 
         lax.fori_loop(0, hs, fresh, 0)
-        lax.fori_loop(0, hs, relayed, 0)
+        if hop == 1:
+            each(send_sum, brest)
+            each(send_sum, crest)
+        lax.fori_loop(0, hs // 2, relayed, 0)
+        if hop == 1:
+            each(send_forward, brest)
+            each(send_forward, crest)
+            each(send_forward, anear)
+        lax.fori_loop(hs // 2, hs, relayed, 0)
+        if hop == 1:
+            products(onear)
+            products(anear)
     scan(0, OWN)
     for n in range(SUBS):
         sub = n // 2 + hs * (n % 2)
@@ -518,7 +529,7 @@
             vmem((8, 4, ROWS, T), BF16),
             vmem((8, 2, HALF, T), BF16),
             vmem((8, 4, HALF, T), BF16),
-            vmem((2, 3, THREE, T), BF16),
+            vmem((4, 3, THREE, T), BF16),
             vmem((8, 2, HALF, T), BF16),
             vmem((8, 4, ROWS, T), BF16),
             vmem((2 * NX * RB, T), jnp.int32),
@@ -532,7 +543,7 @@
             sem((3, 2)), sem((3, 2)), sem((4, 2)), sem((4, 2)),
             sem((7,)), sem((7,)), sem((8,)), sem((2,)),
             sem((2, NZ)), sem((2, NZ)), sem((16, 12)), sem((16, 12)),
-            sem((3,)), sem((2, 4, SUBS)), sem((2, 4, SUBS)),
+            sem((4,)), sem((2, 4, SUBS)), sem((2, 4, SUBS)),
         ],
         compiler_params=pltpu.CompilerParams(
             collective_id=0, has_side_effects=True, vmem_limit_bytes=VMEM_MIB << 20),

time: 109 us -> 105 us (0.963); the launches traced: 109 us -> 104 us
  Pallas kernels: 106 us -> 101 us
    pallas_call x1, Pallas kernels: 106 us -> 101 us  [local(): pl.pallas_call(step, out_shape=jax.ShapeDtypeStruct((Q, 64 * T), F32), in...]
where the time goes in v4:
time: 105 us; the launch traced here: 104 us
  Pallas kernels  101 us (96%)
  local copies, waits for them, and re-layouts  2.79 us (3%)
    pallas_call x1, Pallas kernels, local(): pl.pallas_call(step, out_shape=jax.ShapeDtypeStruct((Q, 64 * T), F32), in...  101 us
    unnamed x5, local copies, waits for them, and re-layouts  2.79 us

profile of v4, /device:TPU:1, one launch (start us, length us, event | category | flops | bytes accessed | tf_op | source)
XLA Modules:
  0.0 103.8 jit_solution(4465965216687868298)
XLA Ops:
  0.0 0.0 copy-start
  0.0 1.1 %copy-done = bf16[1,4,1,6,128,128]{5,4,3,2,1,0:T(8,128)(2,1)S(1)} copy-done((bf16[1,4,1,6,128,128]{5,4,3,2,1,0:T(8,128)(2,1)S(1)}, bf16[1,4,1,6,128,128]{5,4,3,2,1,0:T(8,128)(2,1)}, u32[]{:S(2)}) %copy-start) | copy-done | bytes 786456
  1.1 0.0 copy-start.1
  1.1 0.7 copy-done.1
  1.8 101.0 %step.1 = f32[32,8192]{1,0:T(8,128)S(1)} custom-call(bf16[4,6,128,128]{3,2,1,0:T(8,128)(2,1)S(1)} %bitcast.1, s32[1,4,1,6]{3,2,1,0:T(1,128)S(1)} %copy-done.1), custom_call_target="tpu_custom_call" | custom-call | tf_op jit(solution)/shard_map/step/pallas_call | solution.py:514
  102.8 1.0 copy.4
Async XLA Ops:
  0.0 1.1 %copy-start = (bf16[1,4,1,6,128,128]{5,4,3,2,1,0:T(8,128)(2,1)S(1)}, bf16[1,4,1,6,128,128]{5,4,3,2,1,0:T(8,128)(2,1)}, u32[]{:S(2)}) copy-start(bf16[1,4,1,6,128,128]{5,4,3,2,1,0:T(8,128)(2,1)} %param.2) | copy-start | bytes 2359300
  1.1 0.7 copy-start.1

commit v5 on v4

--- a/solution.py
+++ b/solution.py
@@ -382,11 +382,11 @@
     each(send_forward, ofar)
     each(send_forward, afar)
     squares(brest, send=False)
+    products(bfar)
     each(send_sum_direct, cfar)
     each(send_parts, brest)
+    squares(crest)
     products(ofar)
-    products(bfar)
-    squares(crest)
     products(afar)
     order_copy.wait()
 
@@ -394,24 +394,26 @@
     ahead = lax.rem(y - x + NX, NX)
     here = jnp.where(ahead == 0, 0, jnp.where(ahead == 3, 1, jnp.where(ahead == 1, 2, 3)))
 
-    def scan(way, p):
-        rows = slice(p * Q, p * Q + Q)
-        run = jnp.zeros((Q, T), F32)
+    def scan(*windows):
+        spans = [slice(p * Q, p * Q + Q) for p in windows]
+        runs = tuple(jnp.zeros((Q, T), F32) for p in windows)
         for part in range(2):
-            def body(n, run, part=part):
+            def body(n, runs, part=part):
                 for m in range(8):
                     t = n * 8 + m
                     code = ords[part, 0, t]
-                    tile = prods[code // 2, rows]
-                    run = tile + run * lax.rem(code, 2).astype(F32)
-                    sums[way, part * T + t] = run
-                return run
-
-            run = lax.fori_loop(0, 16 if part == 0 else TILES // 8 - 16, body, run)
+                    keep = lax.rem(code, 2).astype(F32)
+                    runs = tuple(prods[code // 2, rows] + run * keep for rows, run in zip(spans, runs))
+                    for way, run in enumerate(runs):
+                        sums[way, part * T + t] = run
+                return runs
+
+            runs = lax.fori_loop(0, 16 if part == 0 else TILES // 8 - 16, body, runs)
         for n in range(2 * RB):
             last = ords[2, 0, 8 * z + n]
-            mine = sfin[here * 2 + n % 4 // 2, n // 4 * 2 + n % 2, rows].astype(F32)
-            sums[way, TILES + 1 + n] = sums[way, last] - 1.5 * mine
+            for way, rows in enumerate(spans):
+                mine = sfin[here * 2 + n % 4 // 2, n // 4 * 2 + n % 2, rows].astype(F32)
+                sums[way, TILES + 1 + n] = sums[way, last] - 1.5 * mine
 
     def result_tile(way, j):
         own = j - 8 * z
@@ -438,7 +440,7 @@
         sums[way, TILES] = jnp.zeros((Q, T), F32)
     hs = SUBS // 2
     products(cfar)
-    scan(0, 0)
+    scan(0)
 
     def hop0(n, carry):
         emit(0, 0, n, False)
@@ -448,15 +450,17 @@
     lax.fori_loop(0, hs, hop0, 0)
     for hop in range(1, 4):
         if hop == 1:
-            each(send_forward, onear)
-            each(send_sum, anear)
             each(send_relay, brest)
             each(send_relay, crest)
         if hop == 2:
             products(brest)
             products(crest)
-        scan(0, 2 * hop - 1)
-        scan(1, 2 * hop)
+            each(send_forward, onear)
+            each(send_sum, anear)
+        if hop == 3:
+            products(onear)
+            products(anear)
+        scan(2 * hop - 1, 2 * hop)
 
         def fresh(n, carry, hop=hop):
             emit(0, hop, n + hs, hop > 1, hop == 3)
@@ -476,12 +480,10 @@
         if hop == 1:
             each(send_forward, brest)
             each(send_forward, crest)
+        if hop == 2:
             each(send_forward, anear)
         lax.fori_loop(hs // 2, hs, relayed, 0)
-        if hop == 1:
-            products(onear)
-            products(anear)
-    scan(0, OWN)
+    scan(OWN)
     for n in range(SUBS):
         sub = n // 2 + hs * (n % 2)
         for way in range(2):

time: 105 us -> 102 us (0.971)
  Pallas kernels: 101 us -> 98.8 us
    pallas_call x1, Pallas kernels: 101 us -> 98.8 us  [local(): pl.pallas_call(step, out_shape=jax.ShapeDtypeStruct((Q, 64 * T), F32), in...]
where the time goes in v5:
time: 102 us
  Pallas kernels  98.8 us (97%)
  local copies, waits for them, and re-layouts  2.79 us (3%)
    pallas_call x1, Pallas kernels, local(): pl.pallas_call(step, out_shape=jax.ShapeDtypeStruct((Q, 64 * T), F32), in...  98.8 us
    unnamed x5, local copies, waits for them, and re-layouts  2.79 us

profile of v5, /device:TPU:1, one launch (start us, length us, event | category | flops | bytes accessed | tf_op | source)
XLA Modules:
  0.0 101.6 jit_solution(3789553974169015922)
XLA Ops:
  0.0 0.0 copy-start
  0.0 1.1 %copy-done = bf16[1,4,1,6,128,128]{5,4,3,2,1,0:T(8,128)(2,1)S(1)} copy-done((bf16[1,4,1,6,128,128]{5,4,3,2,1,0:T(8,128)(2,1)S(1)}, bf16[1,4,1,6,128,128]{5,4,3,2,1,0:T(8,128)(2,1)}, u32[]{:S(2)}) %copy-start) | copy-done | bytes 786456
  1.1 0.0 copy-start.1
  1.1 0.7 copy-done.1
  1.8 98.8 %step.1 = f32[32,8192]{1,0:T(8,128)S(1)} custom-call(bf16[4,6,128,128]{3,2,1,0:T(8,128)(2,1)S(1)} %bitcast.1, s32[1,4,1,6]{3,2,1,0:T(1,128)S(1)} %copy-done.1), custom_call_target="tpu_custom_call" | custom-call | tf_op jit(solution)/shard_map/step/pallas_call | solution.py:516
  100.6 1.0 copy.4
Async XLA Ops:
  0.0 1.1 %copy-start = (bf16[1,4,1,6,128,128]{5,4,3,2,1,0:T(8,128)(2,1)S(1)}, bf16[1,4,1,6,128,128]{5,4,3,2,1,0:T(8,128)(2,1)}, u32[]{:S(2)}) copy-start(bf16[1,4,1,6,128,128]{5,4,3,2,1,0:T(8,128)(2,1)} %param.2) | copy-start | bytes 2359300
  1.1 0.7 copy-start.1
